TPU v7x, 32 devices: a whole 2x2x4 slice. The times are simulated.
32 devices in a mesh: row: 4 (over z), col: 8 (over y, x, core).
Axes of the slice: x: 2, y: 2, z: 4, core: 2. Of those that a mesh axis runs over, the one named last changes fastest.
Arguments:
- band_sites: float32 [2, 128], P(None, 'row'), may hold values from 0 to 1
- test_sites: float32 [2, 1024], P(None, 'col'), may hold values from 0 to 1
- band_factor: float32 [128, 128], P('row', 'col'), as said below
- prior_factor: float32 [128, 2048], P('row', 'col'), may hold values from -0.125 to 0.125
- prior_solution: float32 [2048, 1024], P('col', 'row'), may hold values from -6 to 6
- prior_covariance: float32 [1024, 1024], P('row', 'col'), may hold values from -4 to 4
Outputs:
- band_solution: float32 [128, 1024], P('row', 'col')
- covariance: float32 [1024, 1024], P('row', 'col')
Inputs may be any that keep to these rules, and one draw needn't show every extreme that they name: band_factor is lower triangular with diagonal entries in 1 to 2 and small entries below it.
All inputs are finite; a program needn't handle non-finite values.
Results may differ from a plain program's by a relative error of at most 0.00011.
Values sent between devices are 32-bit elements; how exact they have to be, the bound alone decides.
No kernel may reach another device: no remote copies, remote signals or barrier semaphores. Data moves between devices by JAX's collectives and lax.ppermute only.
A program may use at most 64 MiB of HBM per device.

v0:
```python
import jax
import jax.numpy as jnp
from jax import lax
from jax.sharding import PartitionSpec as P

length_scale = 0.3


def matern(band_sites, test_sites):
    delta_x = band_sites[0][:, None] - test_sites[0][None, :]
    delta_y = band_sites[1][:, None] - test_sites[1][None, :]
    scaled = jnp.sqrt(delta_x * delta_x + delta_y * delta_y + 1e-06) * (3.0**0.5 / length_scale)
    return (1.0 + scaled) * jnp.exp(-scaled)


def local(band_sites, test_sites, band_factor, prior_factor, prior_solution, prior_covariance):
    tile_rows = band_factor.shape[0]
    test_cols = test_sites.shape[1]
    row_count = lax.axis_size("row")
    my_row = lax.axis_index("row")
    cross = matern(band_sites, test_sites)
    partial_terms = lax.dot_general(
        lax.all_gather(prior_solution, "row", axis=1, tiled=True),
        prior_factor,
        (((0,), (1,)), ((), ())),
        precision=lax.Precision.HIGHEST,
        preferred_element_type=jnp.float32,
    )
    update = lax.psum_scatter(partial_terms, "col", scatter_dimension=0, tiled=True)
    remaining = cross - update.T
    factor_row = lax.all_gather(band_factor, "col", axis=1, tiled=True)
    whole_rest = lax.all_gather(remaining, "row", axis=0, tiled=True)
    whole_factor = lax.all_gather(factor_row, "row", axis=0, tiled=True)
    whole_solved = lax.linalg.triangular_solve(whole_factor, whole_rest, left_side=True, lower=True)
    collected = whole_solved.reshape(row_count, tile_rows, test_cols)
    band_solution = lax.dynamic_index_in_dim(collected, my_row, 0, keepdims=False)
    band_rows = lax.all_gather(band_solution, "col", axis=1, tiled=True)
    gram_sum = lax.psum_scatter(
        lax.dot_general(
            band_rows,
            band_solution,
            (((0,), (0,)), ((), ())),
            precision=lax.Precision.HIGHEST,
            preferred_element_type=jnp.float32,
        ),
        "row",
        scatter_dimension=0,
        tiled=True,
    )
    return (band_solution, prior_covariance - gram_sum)


def solution(mesh):
    placed = (
        P(None, "row"),
        P(None, "col"),
        P("row", "col"),
        P("row", "col"),
        P("col", "row"),
        P("row", "col"),
    )
    return jax.shard_map(
        local,
        mesh=mesh,
        in_specs=placed,
        out_specs=(P("row", "col"), P("row", "col")),
        check_vma=False,
    )
```

profile of v0, /device:TPU:0, one launch (start us, length us, event | category | flops | bytes accessed | tf_op | source)
XLA Modules:
  0.0 136.1 jit_solution(165506387914576891)
XLA Ops:
  7.2 0.0 copy-start
  7.2 0.0 all-gather.3.cloned.1.call-start
  7.2 0.7 all-gather.3.cloned.1.call-update
  7.9 0.0 reduce-scatter.3.cloned.1.call-start
  8.0 0.6 copy-done.3
  8.6 10.7 %all_gather.15 = f32[32,128]{0,1:T(8,128)S(1)} all-gather(f32[32,16]{0,1:T(8,128)S(1)} %copy-done.3), channel_id=1, replica_groups=mesh['row'=4,'col'=8] {'col'}, dimensions={1}, use_global_device_ids=true | all-gather | bytes 18432 | tf_op jit(solution)/shard_map/all_gather | solution.py:31
  19.3 0.1 copy.12
  19.4 14.0 %all_gather.16 = f32[128,128]{1,0:T(8,128)S(1)} all-gather(f32[32,128]{1,0:T(8,128)S(1)} %copy.12), channel_id=1, replica_groups=mesh['row'=4,'col'=8] {'row'}, dimensions={0}, use_global_device_ids=true | all-gather | bytes 81920 | tf_op jit(solution)/shard_map/all_gather | solution.py:33
  33.4 9.8 %custom-call.3 = f32[1,128,128]{1,2,0:T(8,128)S(1)} custom-call(f32[1,128,128]{2,1,0:T(8,128)S(1)} %select_bitcast_fusion), custom_call_target="InvertDiagBlocksLowerTriangular" | custom-call | tf_op jit(solution)/shard_map/triangular_solve | solution.py:34
  43.2 0.1 copy.13
  43.3 0.7 copy-done.4
  44.0 2.6 %fusion.4 = f32[1024,32]{0,1:T(8,128)} fusion(f32[256,1024]{1,0:T(8,128)} %all-gather.3.cloned.1.call-done, f32[32,256]{1,0:T(8,128)S(1)} %copy-done), kind=kOutput, calls=%fused_computation.12 | convolution fusion | flops 100663296 | bytes 1212416 | tf_op jit(solution)/shard_map/dot_general | solution.py:22
  46.6 0.0 reduce-scatter.3.cloned.1.call-update
  46.6 0.0 reduce-scatter.5.cloned.1.call-start
  46.7 0.6 copy-done.5
  47.3 33.4 %reduce-scatter.3.cloned.1.call-done = f32[128,32]{0,1:T(8,128)} async-done(((f32[1024,32]{0,1:T(8,128)}), f32[128,32]{0,1:T(8,128)}) %reduce-scatter.3.cloned.1.call-update) | async-done | bytes 16400 | tf_op jit(solution)/shard_map/reduce_scatter | solution.py:29
  80.7 0.8 bitcast_subtract_fusion
  81.5 13.3 %all_gather.18 = f32[128,128]{1,0:T(8,128)S(1)} all-gather(f32[32,128]{1,0:T(8,128)S(1)} %bitcast_subtract_fusion), channel_id=1, replica_groups=mesh['row'=4,'col'=8] {'row'}, dimensions={0}, use_global_device_ids=true | all-gather | bytes 81920 | tf_op jit(solution)/shard_map/all_gather | solution.py:32
  94.7 0.2 fusion.2
  95.0 9.3 %all-gather = f32[1,32,1024]{2,1,0:T(8,128)S(1)} all-gather(f32[1,32,128]{2,1,0:T(8,128)S(1)} %constant_dynamic-slice_fusion), channel_id=2, replica_groups=mesh['row'=4,'col'=8] {'col'}, dimensions={2}, use_global_device_ids=true | all-gather | bytes 147456 | tf_op jit(solution)/shard_map/all_gather | solution.py:37
  104.3 1.8 %fusion = f32[1024,128]{1,0:T(8,128)} fusion(f32[32,128]{1,0:T(8,128)S(1)} %fusion.9, f32[1,32,1024]{2,1,0:T(8,128)S(1)} %all-gather), kind=kOutput, calls=%fused_computation | convolution fusion | flops 50331648 | bytes 671744 | tf_op jit(solution)/shard_map/dot_general | solution.py:39
  106.0 0.0 reduce-scatter.5.cloned.1.call-update
  106.1 21.9 %reduce-scatter.5.cloned.1.call-done = f32[256,128]{1,0:T(8,128)} async-done(((f32[1024,128]{1,0:T(8,128)}), f32[256,128]{1,0:T(8,128)}) %reduce-scatter.5.cloned.1.call-update) | async-done | bytes 131088 | tf_op jit(solution)/shard_map/reduce_scatter | solution.py:38
  128.0 1.6 %sub.51 = f32[256,128]{1,0:T(8,128)} subtract(f32[256,128]{1,0:T(8,128)S(1)} %copy-done.1, f32[256,128]{1,0:T(8,128)} %reduce-scatter.5.cloned.1.call-done) | non-fusion elementwise | flops 32768 | bytes 393216 | tf_op jit(solution)/shard_map/sub | solution.py:50
  (14 shorter events, 0.1 us)
Async XLA Ops:
  7.2 36.8 %copy-start = (f32[32,256]{1,0:T(8,128)S(1)}, f32[32,256]{1,0:T(8,128)}, u32[]{:S(2)}) copy-start(f32[32,256]{1,0:T(8,128)} %param.9) | copy-start | bytes 98308
  7.2 36.8 %all-gather.3.cloned.1.call-start = ((), (), s32[]{:S(2)}) async-start(), calls=%async_computation.2 | async-start | bytes 1310720 | tf_op jit(solution)/shard_map/all_gather | solution.py:23
  7.9 0.7 copy-start.3
  7.9 72.7 %reduce-scatter.3.cloned.1.call-start = ((), (), s32[]{:S(2)}) async-start(), calls=%async_computation.3 | async-start | bytes 147456 | tf_op jit(solution)/shard_map/reduce_scatter | solution.py:29
  43.3 0.7 copy-start.4
  46.6 0.7 copy-start.5
  46.6 81.3 %reduce-scatter.5.cloned.1.call-start = ((), (), s32[]{:S(2)}) async-start(), calls=%async_computation.4 | async-start | bytes 655360 | tf_op jit(solution)/shard_map/reduce_scatter | solution.py:38
  95.0 9.3 %copy-start.2 = (f32[32,128]{1,0:T(8,128)}, f32[32,128]{1,0:T(8,128)S(1)}, u32[]{:S(2)}) copy-start(f32[32,128]{1,0:T(8,128)S(1)} %fusion.9) | copy-start | bytes 49156
  106.0 21.9 %copy-start.1 = (f32[256,128]{1,0:T(8,128)S(1)}, f32[256,128]{1,0:T(8,128)}, u32[]{:S(2)}) copy-start(f32[256,128]{1,0:T(8,128)} %param.11) | copy-start | bytes 393220
Sparse Core Ops, SparseCore 0:
  9.6 31.7 all-gather.2
  46.8 33.8 reduce-scatter.2
  106.2 21.7 reduce-scatter.4
where the time goes:
time: 136 us
  waiting for transfers between devices  56 us (41%)
  blocking collectives  47.2 us (35%)
  between operations  13.8 us (10%)
  other arithmetic  12.2 us (9%)
  matrix products  4.6 us (3%)
  local copies, waits for them, and re-layouts  2.12 us (2%)
    reduce_scatter x1, waiting for transfers between devices, local(): lax.psum_scatter(partial_terms, 'col', scatter_dimension=0, tiled=True)  33.4 us
    reduce_scatter x1, waiting for transfers between devices, local(): lax.psum_scatter(lax.dot_general(band_rows, band_solution, (((0,), (0,)),...  21.9 us
    all_gather x1, blocking collectives, local(): whole_factor = lax.all_gather(factor_row, 'row', axis=0, tiled=True)  14 us
    all_gather x1, blocking collectives, local(): whole_rest = lax.all_gather(remaining, 'row', axis=0, tiled=True)  13.3 us
    all_gather x1, blocking collectives, local(): factor_row = lax.all_gather(band_factor, 'col', axis=1, tiled=True)  10.7 us
    another operation x2, other arithmetic, local(): lax.linalg.triangular_solve(whole_factor, whole_rest, left_side=True, low...  9.82 us
    all_gather x1, blocking collectives, local(): band_rows = lax.all_gather(band_solution, 'col', axis=1, tiled=True)  9.25 us
  transfers between devices with their start and end apart: 3, of which 2 were waited for; matrix products, arithmetic and copies ran while one was open for 7% of the time, Pallas kernels for 0%

commit v1 on v0

v1 whole, which is shorter than its diff:
```python
import jax
import jax.numpy as jnp
from jax import lax
from jax.sharding import PartitionSpec as P

length_scale = 0.3
HIGHEST = lax.Precision.HIGHEST


def matern(band_sites, test_sites):
    delta_x = band_sites[0][:, None] - test_sites[0][None, :]
    delta_y = band_sites[1][:, None] - test_sites[1][None, :]
    scaled = jnp.sqrt(delta_x * delta_x + delta_y * delta_y + 1e-06) * (3.0**0.5 / length_scale)
    return (1.0 + scaled) * jnp.exp(-scaled)


def dot(a, b, contract=((1,), (0,))):
    return lax.dot_general(a, b, (contract, ((), ())), precision=HIGHEST, preferred_element_type=jnp.float32)


def permute(x, rows, cols, target):
    pairs = []
    for r in range(rows):
        for c in range(cols):
            to_r, to_c = target(r, c)
            pairs.append((r * cols + c, to_r * cols + to_c))
    return lax.ppermute(x, ("row", "col"), pairs)


def stages(count):
    out, stride = [], 1
    while stride < count:
        radix = 4 if stride * 4 <= count else 2
        out.append((stride, radix))
        stride *= radix
    return out


def natural(blocks, index):
    count = blocks.shape[0]
    bit = 1
    while bit < count:
        split = blocks.reshape((count // (2 * bit), 2, bit) + blocks.shape[1:])
        blocks = jnp.where((index & bit) != 0, split[:, ::-1], split).reshape(blocks.shape)
        bit *= 2
    return blocks


def gather(x, rows, cols, count, step):
    blocks = x[None]
    for stride, radix in stages(count):
        blocks = jnp.concatenate([blocks] + [permute(blocks, rows, cols, step(d * stride)) for d in range(1, radix)])
    return blocks


def reduce_all(x, rows, cols, count, step):
    for stride, radix in stages(count):
        x = sum([permute(x, rows, cols, step(d * stride)) for d in range(1, radix)], x)
    return x


def lower_inverse(t):
    size = t.shape[0]
    row = lax.broadcasted_iota(jnp.int32, t.shape, 0)
    col = lax.broadcasted_iota(jnp.int32, t.shape, 1)
    inverse = jnp.where(row == col, 1.0 / t, 0.0)
    block = 1
    while block < size:
        below = (row // (2 * block) == col // (2 * block)) & (row // block > col // block)
        inverse = inverse - dot(dot(inverse, jnp.where(below, t, 0.0)), inverse)
        block *= 2
    return inverse


def local(band_sites, test_sites, band_factor, prior_factor, prior_solution, prior_covariance):
    rows, cols = lax.axis_size("row"), lax.axis_size("col")
    tile = test_sites.shape[1]
    band = band_factor.shape[0] * rows
    r, c = lax.axis_index("row"), lax.axis_index("col")
    q, k = c // 2, c % 2

    def along_row(d):
        return lambda i, j: (i ^ d, j)

    def along_col(d):
        return lambda i, j: (i, j ^ (2 * d))

    def other_core(i, j):
        return i, j ^ 1

    factor = natural(gather(prior_factor, rows, cols, rows, along_row), r).reshape(band, -1)
    t_row = natural(gather(band_factor, rows, cols, rows, along_row), r).reshape(band, -1)
    sites = natural(gather(band_sites, rows, cols, rows, along_row), r).transpose(1, 0, 2).reshape(2, band)

    halves = prior_solution.reshape(-1, 2, tile)
    mine = dot(factor, lax.dynamic_index_in_dim(halves, k, 1, keepdims=False))
    theirs = dot(factor, lax.dynamic_index_in_dim(halves, 1 - k, 1, keepdims=False))
    part = mine + permute(theirs, rows, cols, other_core)
    cross = jnp.where(q == r, matern(sites, test_sites), 0.0)
    rest = reduce_all(cross - part, rows, cols, cols // 2, along_col)

    t_pair = jnp.stack([t_row, permute(t_row, rows, cols, other_core)])
    t_pair = natural(t_pair, k).transpose(1, 0, 2).reshape(band, -1)
    t_full = natural(gather(t_pair, rows, cols, cols // 2, along_col), q).transpose(1, 0, 2).reshape(band, band)

    rest_other = permute(rest, rows, cols, other_core)
    moved = permute(rest, rows, cols, lambda i, j: ((j // 2) ^ (rows - 1), 2 * i + j % 2))
    rest_c = jnp.where(q == r, rest, moved)
    inverse = lower_inverse(t_full)
    both = natural(jnp.stack([rest, rest_other]), k)
    left = jnp.concatenate([dot(inverse, both[0]), dot(inverse, both[1])], axis=1)
    right = dot(inverse, rest_c)
    band_solution = lax.dynamic_slice_in_dim(right, r * (band // rows), band // rows, 0)
    return band_solution, prior_covariance - dot(left, right, ((0,), (0,)))


def solution(mesh):
    placed = (
        P(None, "row"),
        P(None, "col"),
        P("row", "col"),
        P("row", "col"),
        P("col", "row"),
        P("row", "col"),
    )
    return jax.shard_map(
        local,
        mesh=mesh,
        in_specs=placed,
        out_specs=(P("row", "col"), P("row", "col")),
        check_vma=False,
    )
```

time: 136 us -> 50.7 us (0.37)
  blocking collectives: 47.2 us -> 0 us
  waiting for transfers between devices: 56 us -> 11.4 us
  starting transfers between devices: 0.12 us -> 27.7 us
  between operations: 13.8 us -> 1.08 us
  other arithmetic: 12.2 us -> 0.41 us
  local copies, waits for them, and re-layouts: 2.12 us -> 3.84 us
  matrix products: 4.6 us -> 6.07 us
    reduce_scatter x2 -> x0, waiting for transfers between devices: 55.2 us -> none  [the longest x1 33.4 us: local(): lax.psum_scatter(partial_terms, 'col', scatter_dimension=0, tiled=True)]
    all_gather x4 -> x0, blocking collectives: 47.2 us -> none  [the longest x1 14 us: local(): whole_factor = lax.all_gather(factor_row, 'row', axis=0, tiled=True)]
    ppermute x0 -> x19, starting transfers between devices: none -> 27.7 us  [permute(): return lax.ppermute(x, ('row', 'col'), pairs)]
    ppermute x0 -> x19, waiting for transfers between devices: none -> 11.4 us  [permute(): return lax.ppermute(x, ('row', 'col'), pairs)]
    another operation x2 -> x6, other arithmetic: 9.82 us -> 0.07 us  [the longest x4 0.05 us: natural(): split = blocks.reshape((count // (2 * bit), 2, bit) + blocks.shape[1:])]
    sub x2 -> x1, other arithmetic: 2.38 us -> 0.01 us  [lower_inverse(): row // (2 * block) == col // (2 * block)]
    dot_general x2 -> x20, matrix products: 4.39 us -> 6.07 us  [dot(): lax.dot_general(a, b, (contract, ((), ())), precision=HIGHEST, preferred_...]
  transfers between devices with their start and end apart: 3 -> 19, of which waited for: 2 -> 10; matrix products, arithmetic and copies ran while one was open for 7% -> 13% of each run, Pallas kernels for 0% -> 0%
where the time goes in v1:
time: 50.7 us; the launch traced here: 50.5 us
  starting transfers between devices  27.7 us (55%)
  waiting for transfers between devices  11.4 us (22%)
  matrix products  6.07 us (12%)
  local copies, waits for them, and re-layouts  3.84 us (8%)
  between operations  1.08 us (2%)
    ppermute x19, starting transfers between devices, permute(): return lax.ppermute(x, ('row', 'col'), pairs)  27.7 us
    ppermute x19, waiting for transfers between devices, permute(): return lax.ppermute(x, ('row', 'col'), pairs)  11.4 us
    dot_general x20, matrix products, dot(): lax.dot_general(a, b, (contract, ((), ())), precision=HIGHEST, preferred_...  6.07 us
    unnamed x10, local copies, waits for them, and re-layouts  1.36 us
    reshape x1, local copies, waits for them, and re-layouts, local(): halves = prior_solution.reshape(-1, 2, tile)  1.08 us
  transfers between devices with their start and end apart: 19, of which 10 were waited for; matrix products, arithmetic and copies ran while one was open for 13% of the time, Pallas kernels for 0%

profile of v1, /device:TPU:0, one launch (start us, length us, event | category | flops | bytes accessed | tf_op | source)
XLA Modules:
  0.0 50.5 jit_solution(11956175597692227139)
XLA Ops:
  0.6 3.1 %collective-permute-start.10 = (f32[1,32,256]{2,1,0:T(8,128)}, f32[1,32,256]{2,1,0:T(8,128)S(1)}, u32[]{:S(2)}, u32[]{:S(2)}) collective-permute-start(f32[1,32,256]{2,1,0:T(8,128)} %bitcast.100), channel_id=1, source_target_pairs={{0,8},{1,9},{2,10},{3,11},{4,12},{5,13},{6,14},{7,15},{8,0},{9,1},... | collective-permute-start | bytes 98312 | tf_op jit(solution)/shard_map/ppermute | solution.py:27
  3.8 2.6 %collective-permute-start.11 = (f32[1,32,256]{2,1,0:T(8,128)}, f32[1,32,256]{2,1,0:T(8,128)S(1)}, u32[]{:S(2)}, u32[]{:S(2)}) collective-permute-start(f32[1,32,256]{2,1,0:T(8,128)} %bitcast.101), channel_id=1, source_target_pairs={{0,16},{1,17},{2,18},{3,19},{4,20},{5,21},{6,22},{7,23},{8,24},{9,... | collective-permute-start | bytes 98312 | tf_op jit(solution)/shard_map/ppermute | solution.py:27
  6.3 0.4 collective-permute-start.7
  7.0 3.8 %collective-permute-start.9 = (f32[1,2,32]{2,1,0:T(2,128)S(1)}, f32[1,2,32]{2,1,0:T(2,128)S(1)}, u32[]{:S(2)}, u32[]{:S(2)}) collective-permute-start(f32[1,2,32]{2,1,0:T(2,128)S(1)} %bitcast.113), channel_id=1, source_target_pairs={{0,24},{1,25},{2,26},{3,27},{4,28},{5,29},{6,30},{7,31},{8,16},{9,... | collective-permute-start | bytes 776 | tf_op jit(solution)/shard_map/ppermute | solution.py:27
  10.9 1.1 %reshape.134 = f32[256,2,128]{2,1,0:T(2,128)S(1)} reshape(f32[256,256]{1,0:T(8,128)} %param.10) | data formatting | bytes 524288 | tf_op jit(solution)/shard_map/reshape | solution.py:95
  12.0 0.7 %copy-done.3 = f32[2,128]{1,0:T(2,128)S(1)} copy-done((f32[2,128]{1,0:T(2,128)S(1)}, f32[2,128]{1,0:T(2,128)}, u32[]{:S(2)}) %copy-start.3) | copy-done | bytes 1048
  12.9 0.7 %copy-done.2 = f32[32,16]{0,1:T(8,128)S(1)} copy-done((f32[32,16]{0,1:T(8,128)S(1)}, f32[32,16]{0,1:T(8,128)}, u32[]{:S(2)}) %copy-start.2) | copy-done | bytes 2072
  13.6 0.6 %collective-permute-start.1 = (f32[1,32,16]{1,2,0:T(8,128)S(1)}, f32[1,32,16]{1,2,0:T(8,128)S(1)}, u32[]{:S(2)}, u32[]{:S(2)}) collective-permute-start(f32[1,32,16]{1,2,0:T(8,128)S(1)} %bitcast.108), channel_id=1, source_target_pairs={{0,16},{1,17},{2,18},{3,19},{4,20},{5,21},{6,22},{7,23},{8,24},{9,... | collective-permute-start | bytes 6152 | tf_op jit(solution)/shard_map/ppermute | solution.py:27
  14.2 3.8 %collective-permute-start.2 = (f32[1,32,16]{1,2,0:T(8,128)S(1)}, f32[1,32,16]{1,2,0:T(8,128)S(1)}, u32[]{:S(2)}, u32[]{:S(2)}) collective-permute-start(f32[1,32,16]{1,2,0:T(8,128)S(1)} %bitcast.109), channel_id=1, source_target_pairs={{0,24},{1,25},{2,26},{3,27},{4,28},{5,29},{6,30},{7,31},{8,16},{9,... | collective-permute-start | bytes 6152 | tf_op jit(solution)/shard_map/ppermute | solution.py:27
  18.2 1.5 %collective-permute-done.2 = f32[1,32,16]{1,2,0:T(8,128)S(1)} collective-permute-done((f32[1,32,16]{1,2,0:T(8,128)S(1)}, f32[1,32,16]{1,2,0:T(8,128)S(1)}, u32[]{:S(2)}, u32[]{:S(2)}) %collective-permute-start.2) | collective-permute-done | bytes 2080 | tf_op jit(solution)/shard_map/ppermute | solution.py:27
  20.1 1.0 %collective-permute-done.3 = f32[128,16]{0,1:T(8,128)S(1)} collective-permute-done((f32[128,16]{0,1:T(8,128)S(1)}, f32[128,16]{0,1:T(8,128)S(1)}, u32[]{:S(2)}, u32[]{:S(2)}) %collective-permute-start.3) | collective-permute-done | bytes 8224 | tf_op jit(solution)/shard_map/ppermute | solution.py:27
  21.2 1.7 %collective-permute-start.4 = (f32[1,128,32]{1,2,0:T(8,128)S(1)}, f32[1,128,32]{1,2,0:T(8,128)S(1)}, u32[]{:S(2)}, u32[]{:S(2)}) collective-permute-start(f32[1,128,32]{1,2,0:T(8,128)S(1)} %bitcast.96), channel_id=1, source_target_pairs={{0,2},{1,3},{2,0},{3,1},{4,6},{5,7},{6,4},{7,5},{8,10},{9,11},{10,... | collective-permute-start | bytes 49160 | tf_op jit(solution)/shard_map/ppermute | solution.py:27
  22.9 1.5 %collective-permute-start.5 = (f32[1,128,32]{1,2,0:T(8,128)S(1)}, f32[1,128,32]{1,2,0:T(8,128)S(1)}, u32[]{:S(2)}, u32[]{:S(2)}) collective-permute-start(f32[1,128,32]{1,2,0:T(8,128)S(1)} %bitcast.97), channel_id=1, source_target_pairs={{0,4},{1,5},{2,6},{3,7},{4,0},{5,1},{6,2},{7,3},{8,12},{9,13},{10,... | collective-permute-start | bytes 49160 | tf_op jit(solution)/shard_map/ppermute | solution.py:27
  25.0 3.7 %collective-permute-start.12 = (f32[1,32,256]{2,1,0:T(8,128)S(1)}, f32[1,32,256]{2,1,0:T(8,128)S(1)}, u32[]{:S(2)}, u32[]{:S(2)}) collective-permute-start(f32[1,32,256]{2,1,0:T(8,128)S(1)} %bitcast.102), channel_id=1, source_target_pairs={{0,24},{1,25},{2,26},{3,27},{4,28},{5,29},{6,30},{7,31},{8,16},{9,... | collective-permute-start | bytes 98312 | tf_op jit(solution)/shard_map/ppermute | solution.py:27
  33.2 1.0 %collective-permute-done.13 = f32[128,128]{1,0:T(8,128)S(1)} collective-permute-done((f32[128,128]{1,0:T(8,128)S(1)}, f32[128,128]{1,0:T(8,128)S(1)}, u32[]{:S(2)}, u32[]{:S(2)}) %collective-permute-start.13) | collective-permute-done | bytes 65568 | tf_op jit(solution)/shard_map/ppermute | solution.py:27
  34.5 1.3 %collective-permute-start.14 = (f32[128,128]{1,0:T(8,128)S(1)}, f32[128,128]{1,0:T(8,128)S(1)}, u32[]{:S(2)}, u32[]{:S(2)}) collective-permute-start(f32[128,128]{1,0:T(8,128)S(1)} %fusion), channel_id=1, source_target_pairs={{0,2},{1,3},{2,0},{3,1},{4,6},{5,7},{6,4},{7,5},{8,10},{9,11},{10,... | collective-permute-start | bytes 196616 | tf_op jit(solution)/shard_map/ppermute | solution.py:27
  35.7 1.5 %collective-permute-start.15 = (f32[128,128]{1,0:T(8,128)S(1)}, f32[128,128]{1,0:T(8,128)S(1)}, u32[]{:S(2)}, u32[]{:S(2)}) collective-permute-start(f32[128,128]{1,0:T(8,128)S(1)} %fusion), channel_id=1, source_target_pairs={{0,4},{1,5},{2,6},{3,7},{4,0},{5,1},{6,2},{7,3},{8,12},{9,13},{10,... | collective-permute-start | bytes 196616 | tf_op jit(solution)/shard_map/ppermute | solution.py:27
  37.2 0.8 %collective-permute-start.16 = (f32[128,128]{1,0:T(8,128)S(1)}, f32[128,128]{1,0:T(8,128)S(1)}, u32[]{:S(2)}, u32[]{:S(2)}) collective-permute-start(f32[128,128]{1,0:T(8,128)S(1)} %fusion), channel_id=1, source_target_pairs={{0,6},{1,7},{2,4},{3,5},{4,2},{5,3},{6,0},{7,1},{8,14},{9,15},{10,... | collective-permute-start | bytes 196616 | tf_op jit(solution)/shard_map/ppermute | solution.py:27
  38.8 1.2 %collective-permute-done.15 = f32[128,128]{1,0:T(8,128)S(1)} collective-permute-done((f32[128,128]{1,0:T(8,128)S(1)}, f32[128,128]{1,0:T(8,128)S(1)}, u32[]{:S(2)}, u32[]{:S(2)}) %collective-permute-start.15) | collective-permute-done | bytes 65568 | tf_op jit(solution)/shard_map/ppermute | solution.py:27
  40.0 2.4 %collective-permute-done.16 = f32[128,128]{1,0:T(8,128)S(1)} collective-permute-done((f32[128,128]{1,0:T(8,128)S(1)}, f32[128,128]{1,0:T(8,128)S(1)}, u32[]{:S(2)}, u32[]{:S(2)}) %collective-permute-start.16) | collective-permute-done | bytes 65568 | tf_op jit(solution)/shard_map/ppermute | solution.py:27
  42.7 2.2 %collective-permute-start.17 = (f32[128,128]{1,0:T(8,128)S(1)}, f32[128,128]{1,0:T(8,128)S(1)}, u32[]{:S(2)}, u32[]{:S(2)}) collective-permute-start(f32[128,128]{1,0:T(8,128)S(1)} %add_add_fusion), channel_id=1, source_target_pairs={{0,24},{1,25},{2,16},{3,17},{4,8},{5,9},{6,0},{7,1},{8,26},{9,27},... | collective-permute-start | bytes 196616 | tf_op jit(solution)/shard_map/ppermute | solution.py:27
  45.4 3.2 %collective-permute-done.17 = f32[128,128]{1,0:T(8,128)S(1)} collective-permute-done((f32[128,128]{1,0:T(8,128)S(1)}, f32[128,128]{1,0:T(8,128)S(1)}, u32[]{:S(2)}, u32[]{:S(2)}) %collective-permute-start.17) | collective-permute-done | bytes 65568 | tf_op jit(solution)/shard_map/ppermute | solution.py:27
  48.8 0.6 %constant_dynamic-slice_fusion = f32[32,128]{1,0:T(8,128)} fusion(f32[128,128]{1,0:T(8,128)S(1)} %fusion.10, s32[]{:T(128)S(6)} %select_n.291), kind=kLoop, calls=%fused_computation.189 | loop fusion | bytes 32772 | tf_op jit(solution)/shard_map/dynamic_slice | solution.py:113
  49.4 1.0 %convolution_subtract_fusion = f32[256,128]{1,0:T(8,128)} fusion(f32[256,128]{1,0:T(8,128)S(1)} %copy-done, f32[128,128]{1,0:T(8,128)S(1)} %fusion.10, f32[128,128]{1,0:T(8,128)S(1)} %fusion.7, f32[128,128]{1,0:T(8,128)S(1)} %fusion.8), kind=kOutput, calls=%fused_computation | convolution fusion | flops 50397184 | bytes 458752 | tf_op jit(solution)/shard_map/dot_general | solution.py:18
  (89 shorter events, 7.8 us)
Async XLA Ops:
  0.6 5.7 %copy-start.4 = (f32[2,32]{1,0:T(2,128)S(1)}, f32[2,32]{1,0:T(2,128)}, u32[]{:S(2)}) copy-start(f32[2,32]{1,0:T(2,128)} %param.6) | copy-start | bytes 772
  0.6 31.9 %collective-permute-start.10 = (f32[1,32,256]{2,1,0:T(8,128)}, f32[1,32,256]{2,1,0:T(8,128)S(1)}, u32[]{:S(2)}, u32[]{:S(2)}) collective-permute-start(f32[1,32,256]{2,1,0:T(8,128)} %bitcast.100), channel_id=1, source_target_pairs={{0,8},{1,9},{2,10},{3,11},{4,12},{5,13},{6,14},{7,15},{8,0},{9,1},... | collective-permute-start | bytes 98312 | tf_op jit(solution)/shard_map/ppermute | solution.py:27
  3.8 28.8 %collective-permute-start.11 = (f32[1,32,256]{2,1,0:T(8,128)}, f32[1,32,256]{2,1,0:T(8,128)S(1)}, u32[]{:S(2)}, u32[]{:S(2)}) collective-permute-start(f32[1,32,256]{2,1,0:T(8,128)} %bitcast.101), channel_id=1, source_target_pairs={{0,16},{1,17},{2,18},{3,19},{4,20},{5,21},{6,22},{7,23},{8,24},{9,... | collective-permute-start | bytes 98312 | tf_op jit(solution)/shard_map/ppermute | solution.py:27
  6.3 6.6 %collective-permute-start.7 = (f32[1,2,32]{2,1,0:T(2,128)S(1)}, f32[1,2,32]{2,1,0:T(2,128)S(1)}, u32[]{:S(2)}, u32[]{:S(2)}) collective-permute-start(f32[1,2,32]{2,1,0:T(2,128)S(1)} %bitcast.111), channel_id=1, source_target_pairs={{0,8},{1,9},{2,10},{3,11},{4,12},{5,13},{6,14},{7,15},{8,0},{9,1},... | collective-permute-start | bytes 776 | tf_op jit(solution)/shard_map/ppermute | solution.py:27
  6.8 6.8 %collective-permute-start.8 = (f32[1,2,32]{2,1,0:T(2,128)S(1)}, f32[1,2,32]{2,1,0:T(2,128)S(1)}, u32[]{:S(2)}, u32[]{:S(2)}) collective-permute-start(f32[1,2,32]{2,1,0:T(2,128)S(1)} %bitcast.112), channel_id=1, source_target_pairs={{0,16},{1,17},{2,18},{3,19},{4,20},{5,21},{6,22},{7,23},{8,24},{9,... | collective-permute-start | bytes 776 | tf_op jit(solution)/shard_map/ppermute | solution.py:27
  7.0 7.3 %collective-permute-start.9 = (f32[1,2,32]{2,1,0:T(2,128)S(1)}, f32[1,2,32]{2,1,0:T(2,128)S(1)}, u32[]{:S(2)}, u32[]{:S(2)}) collective-permute-start(f32[1,2,32]{2,1,0:T(2,128)S(1)} %bitcast.113), channel_id=1, source_target_pairs={{0,24},{1,25},{2,26},{3,27},{4,28},{5,29},{6,30},{7,31},{8,16},{9,... | collective-permute-start | bytes 776 | tf_op jit(solution)/shard_map/ppermute | solution.py:27
  12.0 0.7 %copy-start.3 = (f32[2,128]{1,0:T(2,128)S(1)}, f32[2,128]{1,0:T(2,128)}, u32[]{:S(2)}) copy-start(f32[2,128]{1,0:T(2,128)} %param.7) | copy-start | bytes 3076
  12.9 0.7 %copy-start.2 = (f32[32,16]{0,1:T(8,128)S(1)}, f32[32,16]{0,1:T(8,128)}, u32[]{:S(2)}) copy-start(f32[32,16]{0,1:T(8,128)} %param.8) | copy-start | bytes 6148
  13.6 4.4 %collective-permute-start = (f32[1,32,16]{1,2,0:T(8,128)S(1)}, f32[1,32,16]{1,2,0:T(8,128)S(1)}, u32[]{:S(2)}, u32[]{:S(2)}) collective-permute-start(f32[1,32,16]{1,2,0:T(8,128)S(1)} %bitcast.107), channel_id=1, source_target_pairs={{0,8},{1,9},{2,10},{3,11},{4,12},{5,13},{6,14},{7,15},{8,0},{9,1},... | collective-permute-start | bytes 6152 | tf_op jit(solution)/shard_map/ppermute | solution.py:27
  13.6 4.6 %collective-permute-start.1 = (f32[1,32,16]{1,2,0:T(8,128)S(1)}, f32[1,32,16]{1,2,0:T(8,128)S(1)}, u32[]{:S(2)}, u32[]{:S(2)}) collective-permute-start(f32[1,32,16]{1,2,0:T(8,128)S(1)} %bitcast.108), channel_id=1, source_target_pairs={{0,16},{1,17},{2,18},{3,19},{4,20},{5,21},{6,22},{7,23},{8,24},{9,... | collective-permute-start | bytes 6152 | tf_op jit(solution)/shard_map/ppermute | solution.py:27
  14.2 5.5 %collective-permute-start.2 = (f32[1,32,16]{1,2,0:T(8,128)S(1)}, f32[1,32,16]{1,2,0:T(8,128)S(1)}, u32[]{:S(2)}, u32[]{:S(2)}) collective-permute-start(f32[1,32,16]{1,2,0:T(8,128)S(1)} %bitcast.109), channel_id=1, source_target_pairs={{0,24},{1,25},{2,26},{3,27},{4,28},{5,29},{6,30},{7,31},{8,16},{9,... | collective-permute-start | bytes 6152 | tf_op jit(solution)/shard_map/ppermute | solution.py:27
  20.0 1.2 %collective-permute-start.3 = (f32[128,16]{0,1:T(8,128)S(1)}, f32[128,16]{0,1:T(8,128)S(1)}, u32[]{:S(2)}, u32[]{:S(2)}) collective-permute-start(f32[128,16]{0,1:T(8,128)S(1)} %reshape_reshape.19), channel_id=1, source_target_pairs={{0,1},{1,0},{2,3},{3,2},{4,5},{5,4},{6,7},{7,6},{8,9},{9,8},{10,11... | collective-permute-start | bytes 24584 | tf_op jit(solution)/shard_map/ppermute | solution.py:27
  21.2 3.8 %copy-start.1 = (f32[32,256]{1,0:T(8,128)S(1)}, f32[32,256]{1,0:T(8,128)}, u32[]{:S(2)}) copy-start(f32[32,256]{1,0:T(8,128)} %param.9) | copy-start | bytes 98308
  21.2 3.8 %collective-permute-start.4 = (f32[1,128,32]{1,2,0:T(8,128)S(1)}, f32[1,128,32]{1,2,0:T(8,128)S(1)}, u32[]{:S(2)}, u32[]{:S(2)}) collective-permute-start(f32[1,128,32]{1,2,0:T(8,128)S(1)} %bitcast.96), channel_id=1, source_target_pairs={{0,2},{1,3},{2,0},{3,1},{4,6},{5,7},{6,4},{7,5},{8,10},{9,11},{10,... | collective-permute-start | bytes 49160 | tf_op jit(solution)/shard_map/ppermute | solution.py:27
  22.9 5.9 %collective-permute-start.5 = (f32[1,128,32]{1,2,0:T(8,128)S(1)}, f32[1,128,32]{1,2,0:T(8,128)S(1)}, u32[]{:S(2)}, u32[]{:S(2)}) collective-permute-start(f32[1,128,32]{1,2,0:T(8,128)S(1)} %bitcast.97), channel_id=1, source_target_pairs={{0,4},{1,5},{2,6},{3,7},{4,0},{5,1},{6,2},{7,3},{8,12},{9,13},{10,... | collective-permute-start | bytes 49160 | tf_op jit(solution)/shard_map/ppermute | solution.py:27
  24.4 4.6 %collective-permute-start.6 = (f32[1,128,32]{1,2,0:T(8,128)S(1)}, f32[1,128,32]{1,2,0:T(8,128)S(1)}, u32[]{:S(2)}, u32[]{:S(2)}) collective-permute-start(f32[1,128,32]{1,2,0:T(8,128)S(1)} %bitcast.98), channel_id=1, source_target_pairs={{0,6},{1,7},{2,4},{3,5},{4,2},{5,3},{6,0},{7,1},{8,14},{9,15},{10,... | collective-permute-start | bytes 49160 | tf_op jit(solution)/shard_map/ppermute | solution.py:27
  25.0 7.6 %collective-permute-start.12 = (f32[1,32,256]{2,1,0:T(8,128)S(1)}, f32[1,32,256]{2,1,0:T(8,128)S(1)}, u32[]{:S(2)}, u32[]{:S(2)}) collective-permute-start(f32[1,32,256]{2,1,0:T(8,128)S(1)} %bitcast.102), channel_id=1, source_target_pairs={{0,24},{1,25},{2,26},{3,27},{4,28},{5,29},{6,30},{7,31},{8,16},{9,... | collective-permute-start | bytes 98312 | tf_op jit(solution)/shard_map/ppermute | solution.py:27
  32.9 1.3 %collective-permute-start.13 = (f32[128,128]{1,0:T(8,128)S(1)}, f32[128,128]{1,0:T(8,128)S(1)}, u32[]{:S(2)}, u32[]{:S(2)}) collective-permute-start(f32[128,128]{1,0:T(8,128)S(1)} %fusion.135), channel_id=1, source_target_pairs={{0,1},{1,0},{2,3},{3,2},{4,5},{5,4},{6,7},{7,6},{8,9},{9,8},{10,11... | collective-permute-start | bytes 196616 | tf_op jit(solution)/shard_map/ppermute | solution.py:27
  34.5 4.3 %collective-permute-start.14 = (f32[128,128]{1,0:T(8,128)S(1)}, f32[128,128]{1,0:T(8,128)S(1)}, u32[]{:S(2)}, u32[]{:S(2)}) collective-permute-start(f32[128,128]{1,0:T(8,128)S(1)} %fusion), channel_id=1, source_target_pairs={{0,2},{1,3},{2,0},{3,1},{4,6},{5,7},{6,4},{7,5},{8,10},{9,11},{10,... | collective-permute-start | bytes 196616 | tf_op jit(solution)/shard_map/ppermute | solution.py:27
  35.7 4.3 %collective-permute-start.15 = (f32[128,128]{1,0:T(8,128)S(1)}, f32[128,128]{1,0:T(8,128)S(1)}, u32[]{:S(2)}, u32[]{:S(2)}) collective-permute-start(f32[128,128]{1,0:T(8,128)S(1)} %fusion), channel_id=1, source_target_pairs={{0,4},{1,5},{2,6},{3,7},{4,0},{5,1},{6,2},{7,3},{8,12},{9,13},{10,... | collective-permute-start | bytes 196616 | tf_op jit(solution)/shard_map/ppermute | solution.py:27
  37.2 5.2 %collective-permute-start.16 = (f32[128,128]{1,0:T(8,128)S(1)}, f32[128,128]{1,0:T(8,128)S(1)}, u32[]{:S(2)}, u32[]{:S(2)}) collective-permute-start(f32[128,128]{1,0:T(8,128)S(1)} %fusion), channel_id=1, source_target_pairs={{0,6},{1,7},{2,4},{3,5},{4,2},{5,3},{6,0},{7,1},{8,14},{9,15},{10,... | collective-permute-start | bytes 196616 | tf_op jit(solution)/shard_map/ppermute | solution.py:27
  42.4 2.5 %collective-permute-start.18 = (f32[128,128]{1,0:T(8,128)S(1)}, f32[128,128]{1,0:T(8,128)S(1)}, u32[]{:S(2)}, u32[]{:S(2)}) collective-permute-start(f32[128,128]{1,0:T(8,128)S(1)} %add_add_fusion), channel_id=1, source_target_pairs={{0,1},{1,0},{2,3},{3,2},{4,5},{5,4},{6,7},{7,6},{8,9},{9,8},{10,11... | collective-permute-start | bytes 196616 | tf_op jit(solution)/shard_map/ppermute | solution.py:27
  42.7 5.9 %collective-permute-start.17 = (f32[128,128]{1,0:T(8,128)S(1)}, f32[128,128]{1,0:T(8,128)S(1)}, u32[]{:S(2)}, u32[]{:S(2)}) collective-permute-start(f32[128,128]{1,0:T(8,128)S(1)} %add_add_fusion), channel_id=1, source_target_pairs={{0,24},{1,25},{2,16},{3,17},{4,8},{5,9},{6,0},{7,1},{8,26},{9,27},... | collective-permute-start | bytes 196616 | tf_op jit(solution)/shard_map/ppermute | solution.py:27
  45.4 4.0 %copy-start = (f32[256,128]{1,0:T(8,128)S(1)}, f32[256,128]{1,0:T(8,128)}, u32[]{:S(2)}) copy-start(f32[256,128]{1,0:T(8,128)} %param.11) | copy-start | bytes 393220

commit v2 on v1

--- a/solution.py
+++ b/solution.py
@@ -53,29 +53,53 @@
     return blocks
 
 
-def reduce_all(x, rows, cols, count, step):
+def reduce_and_gather(x, extra, rows, cols, count, step):
+    blocks, height = extra[None], x.shape[0]
     for stride, radix in stages(count):
-        x = sum([permute(x, rows, cols, step(d * stride)) for d in range(1, radix)], x)
-    return x
+        sent = jnp.concatenate([x, blocks.reshape(-1, x.shape[1])])
+        got = [permute(sent, rows, cols, step(d * stride)) for d in range(1, radix)]
+        x = sum([g[:height] for g in got], x)
+        blocks = jnp.concatenate([blocks] + [g[height:].reshape(blocks.shape) for g in got])
+    return x, blocks
 
 
-def lower_inverse(t):
-    size = t.shape[0]
-    row = lax.broadcasted_iota(jnp.int32, t.shape, 0)
-    col = lax.broadcasted_iota(jnp.int32, t.shape, 1)
-    inverse = jnp.where(row == col, 1.0 / t, 0.0)
+def lower_inverse_t(u):
+    size = u.shape[0]
+    row = lax.broadcasted_iota(jnp.int32, u.shape, 0)
+    col = lax.broadcasted_iota(jnp.int32, u.shape, 1)
+    inverse = jnp.where(row == col, 1.0 / u, 0.0)
     block = 1
     while block < size:
-        below = (row // (2 * block) == col // (2 * block)) & (row // block > col // block)
-        inverse = inverse - dot(dot(inverse, jnp.where(below, t, 0.0)), inverse)
+        above = (row // (2 * block) == col // (2 * block)) & (row // block < col // block)
+        inverse = inverse - dot(dot(inverse, jnp.where(above, u, 0.0)), inverse)
         block *= 2
     return inverse
+
+
+def pack(prior_factor, band_factor, band_sites):
+    width = prior_factor.shape[1]
+    turned = band_factor.T
+    parts = [turned[i : i + 8] for i in range(0, turned.shape[0], 8)]
+    parts.append(jnp.pad(band_sites, ((0, 8 - band_sites.shape[0]), (0, 0))))
+    low = jnp.concatenate(parts, axis=1)
+    low = jnp.pad(low, ((0, 0), (0, width - low.shape[1])))
+    return jnp.concatenate([prior_factor, low])
+
+
+def unpack(blocks, tile_rows, tile_cols):
+    factor = blocks[:, :tile_rows].reshape(-1, blocks.shape[2])
+    low = blocks[:, tile_rows:].transpose(1, 0, 2)
+    lanes = lambda i: low[:, :, i * tile_rows : (i + 1) * tile_rows].reshape(8, -1)
+    groups = tile_cols // 8
+    turned = jnp.concatenate([lanes(i) for i in range(groups)])
+    return factor, turned, lanes(groups)[:2]
 
 
 def local(band_sites, test_sites, band_factor, prior_factor, prior_solution, prior_covariance):
     rows, cols = lax.axis_size("row"), lax.axis_size("col")
     tile = test_sites.shape[1]
-    band = band_factor.shape[0] * rows
+    tile_rows, tile_cols = band_factor.shape
+    band = tile_rows * rows
     r, c = lax.axis_index("row"), lax.axis_index("col")
     q, k = c // 2, c % 2
 
@@ -88,30 +112,31 @@
     def other_core(i, j):
         return i, j ^ 1
 
-    factor = natural(gather(prior_factor, rows, cols, rows, along_row), r).reshape(band, -1)
-    t_row = natural(gather(band_factor, rows, cols, rows, along_row), r).reshape(band, -1)
-    sites = natural(gather(band_sites, rows, cols, rows, along_row), r).transpose(1, 0, 2).reshape(2, band)
+    def to_column(i, j):
+        return (j // 2) ^ (rows - 1) ^ ((i + 1) & (rows // 2)), 2 * i + j % 2
+
+    blocks = natural(gather(pack(prior_factor, band_factor, band_sites), rows, cols, rows, along_row), r)
+    factor, turned, sites = unpack(blocks, tile_rows, tile_cols)
 
     halves = prior_solution.reshape(-1, 2, tile)
+    theirs = dot(factor, lax.dynamic_index_in_dim(halves, 1 - k, 1, keepdims=False))
     mine = dot(factor, lax.dynamic_index_in_dim(halves, k, 1, keepdims=False))
-    theirs = dot(factor, lax.dynamic_index_in_dim(halves, 1 - k, 1, keepdims=False))
-    part = mine + permute(theirs, rows, cols, other_core)
+    turned = turned.reshape(-1, tile)
+    got = permute(jnp.concatenate([theirs, turned]), rows, cols, other_core)
     cross = jnp.where(q == r, matern(sites, test_sites), 0.0)
-    rest = reduce_all(cross - part, rows, cols, cols // 2, along_col)
+    part = (cross - mine) - got[:band]
+    pair = natural(jnp.stack([turned, got[band:]]), k).reshape(-1, tile)
 
-    t_pair = jnp.stack([t_row, permute(t_row, rows, cols, other_core)])
-    t_pair = natural(t_pair, k).transpose(1, 0, 2).reshape(band, -1)
-    t_full = natural(gather(t_pair, rows, cols, cols // 2, along_col), q).transpose(1, 0, 2).reshape(band, band)
-
+    rest, columns = reduce_and_gather(part, pair, rows, cols, cols // 2, along_col)
+    moved = permute(rest, rows, cols, to_column)
     rest_other = permute(rest, rows, cols, other_core)
-    moved = permute(rest, rows, cols, lambda i, j: ((j // 2) ^ (rows - 1), 2 * i + j % 2))
-    rest_c = jnp.where(q == r, rest, moved)
-    inverse = lower_inverse(t_full)
-    both = natural(jnp.stack([rest, rest_other]), k)
-    left = jnp.concatenate([dot(inverse, both[0]), dot(inverse, both[1])], axis=1)
-    right = dot(inverse, rest_c)
-    band_solution = lax.dynamic_slice_in_dim(right, r * (band // rows), band // rows, 0)
-    return band_solution, prior_covariance - dot(left, right, ((0,), (0,)))
+    inverse = lower_inverse_t(natural(columns, q).reshape(band, band))
+    first = ((0,), (0,))
+    both = natural(jnp.stack([dot(inverse, rest, first), dot(inverse, rest_other, first)]), k)
+    right = dot(inverse, jnp.where(q == r, rest, moved), first)
+    left = jnp.concatenate([both[0], both[1]], axis=1)
+    band_solution = lax.dynamic_slice_in_dim(right, r * tile_rows, tile_rows, 0)
+    return band_solution, prior_covariance - dot(left, right, first)
 
 
 def solution(mesh):

time: 50.7 us -> 32 us (0.63)
  starting transfers between devices: 27.7 us -> 10 us
  other arithmetic: 0.41 us -> 1.77 us
  matrix products: 6.07 us -> 5.17 us
  waiting for transfers between devices: 11.4 us -> 10.5 us
  local copies, waits for them, and re-layouts: 3.84 us -> 3.2 us
    ppermute x19 -> x9, starting transfers between devices: 27.7 us -> 10 us  [permute(): return lax.ppermute(x, ('row', 'col'), pairs)]
    unnamed x10 -> x6, local copies, waits for them, and re-layouts: 1.36 us -> 0.02 us
    dot_general x20, matrix products: 6.07 us -> 5.17 us  [dot(): lax.dot_general(a, b, (contract, ((), ())), precision=HIGHEST, preferred_...]
    ppermute x19 -> x9, waiting for transfers between devices: 11.4 us -> 10.5 us  [permute(): return lax.ppermute(x, ('row', 'col'), pairs)]
    slice x0 -> x5, local copies, waits for them, and re-layouts: none -> 0.8 us  [the longest x1 0.71 us: pack(): parts = [turned[i:i + 8] for i in range(0, turned.shape[0], 8)]]
    concatenate x0 -> x4, other arithmetic: none -> 0.78 us  [the longest x1 0.75 us: pack(): low = jnp.concatenate(parts, axis=1)]
    select_n x1 -> x4, other arithmetic: 0.14 us -> 0.77 us  [the longest x3 0.69 us: lower_inverse_t(): inverse = inverse - dot(dot(inverse, jnp.where(above, u, 0.0)), inverse)]
  transfers between devices with their start and end apart: 19 -> 9, of which waited for: 10 -> 7; matrix products, arithmetic and copies ran while one was open for 13% -> 18% of each run, Pallas kernels for 0% -> 0%
where the time goes in v2:
time: 32 us; the launch traced here: 31.7 us
  waiting for transfers between devices  10.5 us (33%)
  starting transfers between devices  10 us (31%)
  matrix products  5.17 us (16%)
  local copies, waits for them, and re-layouts  3.2 us (10%)
  other arithmetic  1.77 us (6%)
  between operations  1.13 us (4%)
    ppermute x9, waiting for transfers between devices, permute(): return lax.ppermute(x, ('row', 'col'), pairs)  10.5 us
    ppermute x9, starting transfers between devices, permute(): return lax.ppermute(x, ('row', 'col'), pairs)  10 us
    dot_general x20, matrix products, dot(): lax.dot_general(a, b, (contract, ((), ())), precision=HIGHEST, preferred_...  5.17 us
    reshape x1, local copies, waits for them, and re-layouts, local(): halves = prior_solution.reshape(-1, 2, tile)  1.09 us
    concatenate x1, other arithmetic, pack(): low = jnp.concatenate(parts, axis=1)  0.75 us
    slice x1, local copies, waits for them, and re-layouts, pack(): parts = [turned[i:i + 8] for i in range(0, turned.shape[0], 8)]  0.71 us
    select_n x3, other arithmetic, lower_inverse_t(): inverse = inverse - dot(dot(inverse, jnp.where(above, u, 0.0)), inverse)  0.69 us
  transfers between devices with their start and end apart: 9, of which 7 were waited for; matrix products, arithmetic and copies ran while one was open for 18% of the time, Pallas kernels for 0%

profile of v2, /device:TPU:0, one launch (start us, length us, event | category | flops | bytes accessed | tf_op | source)
XLA Modules:
  0.0 31.7 jit_solution(10671998315935138816)
XLA Ops:
  0.6 0.7 %fusion.23 = (f32[8,32]{1,0:T(8,128)S(1)}, f32[8,32]{1,0:T(8,128)S(1)}) fusion(f32[16,32]{1,0:T(8,128)} %bitcast.106), kind=kLoop, calls=%fused_computation.126 | loop fusion | bytes 4096 | tf_op jit(solution)/shard_map/slice | solution.py:82
  1.4 0.8 %select_maximum_fusion.1 = f32[8,96]{1,0:T(8,128)S(1)} fusion(f32[2,32]{1,0:T(2,128)} %param.6, f32[8,32]{1,0:T(8,128)S(1)} %get-tuple-element.19, f32[8,32]{1,0:T(8,128)S(1)} %get-tuple-element.18), kind=kLoop, calls=%fused_computation.81 | loop fusion | flops 3072 | bytes 5376 | tf_op jit(solution)/shard_map/concatenate | solution.py:84
  2.1 3.1 %collective-permute-start = (f32[1,40,256]{2,1,0:T(8,128)S(1)}, f32[1,40,256]{2,1,0:T(8,128)S(1)}, u32[]{:S(2)}, u32[]{:S(2)}) collective-permute-start(f32[1,40,256]{2,1,0:T(8,128)S(1)} %fusion.18), channel_id=1, source_target_pairs={{0,8},{1,9},{2,10},{3,11},{4,12},{5,13},{6,14},{7,15},{8,0},{9,1},... | collective-permute-start | bytes 122888 | tf_op jit(solution)/shard_map/ppermute | solution.py:27
  5.2 2.6 %collective-permute-start.1 = (f32[1,40,256]{2,1,0:T(8,128)S(1)}, f32[1,40,256]{2,1,0:T(8,128)S(1)}, u32[]{:S(2)}, u32[]{:S(2)}) collective-permute-start(f32[1,40,256]{2,1,0:T(8,128)S(1)} %fusion.18), channel_id=1, source_target_pairs={{0,16},{1,17},{2,18},{3,19},{4,20},{5,21},{6,22},{7,23},{8,24},{9,... | collective-permute-start | bytes 122888 | tf_op jit(solution)/shard_map/ppermute | solution.py:27
  8.0 1.1 %reshape.192 = f32[256,2,128]{2,1,0:T(2,128)S(1)} reshape(f32[256,256]{1,0:T(8,128)} %param.10) | data formatting | bytes 524288 | tf_op jit(solution)/shard_map/reshape | solution.py:121
  9.4 1.5 %collective-permute-done.1 = f32[1,40,256]{2,1,0:T(8,128)S(1)} collective-permute-done((f32[1,40,256]{2,1,0:T(8,128)S(1)}, f32[1,40,256]{2,1,0:T(8,128)S(1)}, u32[]{:S(2)}, u32[]{:S(2)}) %collective-permute-start.1) | collective-permute-done | bytes 40992 | tf_op jit(solution)/shard_map/ppermute | solution.py:27
  10.9 2.7 %collective-permute-done.2 = f32[1,40,256]{2,1,0:T(8,128)S(1)} collective-permute-done((f32[1,40,256]{2,1,0:T(8,128)S(1)}, f32[1,40,256]{2,1,0:T(8,128)S(1)}, u32[]{:S(2)}, u32[]{:S(2)}) %collective-permute-start.2) | collective-permute-done | bytes 40992 | tf_op jit(solution)/shard_map/ppermute | solution.py:27
  14.1 0.3 fusion.24
  14.6 1.1 %collective-permute-done.3 = f32[144,128]{1,0:T(8,128)S(1)} collective-permute-done((f32[144,128]{1,0:T(8,128)S(1)}, f32[144,128]{1,0:T(8,128)S(1)}, u32[]{:S(2)}, u32[]{:S(2)}) %collective-permute-start.3) | collective-permute-done | bytes 73760 | tf_op jit(solution)/shard_map/ppermute | solution.py:27
  15.7 0.3 slice_subtract_fusion
  16.0 1.6 %collective-permute-start.4 = (f32[160,128]{1,0:T(8,128)S(1)}, f32[160,128]{1,0:T(8,128)S(1)}, u32[]{:S(2)}, u32[]{:S(2)}) collective-permute-start(f32[160,128]{1,0:T(8,128)S(1)} %pad_maximum_fusion.2), channel_id=1, source_target_pairs={{0,2},{1,3},{2,0},{3,1},{4,6},{5,7},{6,4},{7,5},{8,10},{9,11},{10,... | collective-permute-start | bytes 245768 | tf_op jit(solution)/shard_map/ppermute | solution.py:27
  17.6 1.5 %collective-permute-start.5 = (f32[160,128]{1,0:T(8,128)S(1)}, f32[160,128]{1,0:T(8,128)S(1)}, u32[]{:S(2)}, u32[]{:S(2)}) collective-permute-start(f32[160,128]{1,0:T(8,128)S(1)} %pad_maximum_fusion.2), channel_id=1, source_target_pairs={{0,4},{1,5},{2,6},{3,7},{4,0},{5,1},{6,2},{7,3},{8,12},{9,13},{10,... | collective-permute-start | bytes 245768 | tf_op jit(solution)/shard_map/ppermute | solution.py:27
  19.1 0.5 %collective-permute-start.6 = (f32[160,128]{1,0:T(8,128)S(1)}, f32[160,128]{1,0:T(8,128)S(1)}, u32[]{:S(2)}, u32[]{:S(2)}) collective-permute-start(f32[160,128]{1,0:T(8,128)S(1)} %pad_maximum_fusion.2), channel_id=1, source_target_pairs={{0,6},{1,7},{2,4},{3,5},{4,2},{5,3},{6,0},{7,1},{8,14},{9,15},{10,... | collective-permute-start | bytes 245768 | tf_op jit(solution)/shard_map/ppermute | solution.py:27
  19.6 1.0 %collective-permute-done.4 = f32[160,128]{1,0:T(8,128)S(1)} collective-permute-done((f32[160,128]{1,0:T(8,128)S(1)}, f32[160,128]{1,0:T(8,128)S(1)}, u32[]{:S(2)}, u32[]{:S(2)}) %collective-permute-start.4) | collective-permute-done | bytes 81952 | tf_op jit(solution)/shard_map/ppermute | solution.py:27
  20.6 2.3 %collective-permute-done.5 = f32[160,128]{1,0:T(8,128)S(1)} collective-permute-done((f32[160,128]{1,0:T(8,128)S(1)}, f32[160,128]{1,0:T(8,128)S(1)}, u32[]{:S(2)}, u32[]{:S(2)}) %collective-permute-start.5) | collective-permute-done | bytes 81952 | tf_op jit(solution)/shard_map/ppermute | solution.py:27
  22.8 1.6 %collective-permute-done.6 = f32[160,128]{1,0:T(8,128)S(1)} collective-permute-done((f32[160,128]{1,0:T(8,128)S(1)}, f32[160,128]{1,0:T(8,128)S(1)}, u32[]{:S(2)}, u32[]{:S(2)}) %collective-permute-start.6) | collective-permute-done | bytes 81952 | tf_op jit(solution)/shard_map/ppermute | solution.py:27
  24.5 0.6 %collective-permute-start.7 = (f32[128,128]{1,0:T(8,128)S(1)}, f32[128,128]{1,0:T(8,128)S(1)}, u32[]{:S(2)}, u32[]{:S(2)}) collective-permute-start(f32[128,128]{1,0:T(8,128)S(1)} %slice_add_fusion), channel_id=1, source_target_pairs={{0,24},{1,25},{2,16},{3,17},{4,8},{5,9},{6,0},{7,1},{8,10},{9,11},... | collective-permute-start | bytes 196616 | tf_op jit(solution)/shard_map/ppermute | solution.py:27
  25.8 0.4 %bitcast_select_fusion = (f32[128,128]{1,0:T(8,128)S(1)}, f32[128,128]{1,0:T(8,128)S(1)}, f32[128,128]{1,0:T(8,128)S(1)}, f32[128,128]{1,0:T(8,128)S(1)}, f32[128,128]{1,0:T(8,128)S(1)}, /*index=5*/f32[128,128]{1,0:T(8,128)S(1)}) fusion(f32[1,2,2,32,128]{4,3,2,1,0:T(8,128)S(1)} %get-tuple-element.5, s32[128]{0:T(128)S(1)} %get-tuple-element.32, ...), kind=kLoop, calls=%fused_computation.44 | loop fusion | flops 573440 | bytes 465664 | tf_op jit(solution)/shard_map/jit(_where)/select_n | solution.py:74
  28.9 0.3 convolution_bitcast_fusion.1
  29.2 0.3 convolution_bitcast_fusion
  29.6 0.3 collective-permute-done.7
  29.9 0.3 fusion.8
  30.2 0.6 %constant_dynamic-slice_fusion = f32[32,128]{1,0:T(8,128)} fusion(f32[128,128]{1,0:T(8,128)S(1)} %fusion.8, s32[]{:T(128)S(6)} %select_n.263), kind=kLoop, calls=%fused_computation.111 | loop fusion | bytes 32772 | tf_op jit(solution)/shard_map/dynamic_slice | solution.py:138
  30.8 0.9 %convolution_subtract_fusion = f32[256,128]{1,0:T(8,128)} fusion(f32[256,128]{1,0:T(8,128)S(1)} %copy-done, f32[128,128]{1,0:T(8,128)S(1)} %fusion.8, f32[128,128]{0,1:T(8,128)S(1)} %slice_bitcast_fusion, f32[128,128]{0,1:T(8,128)S(1)} %slice_bitcast_fusion.1), kind=kOutput, calls=%fused_computation | convolution fusion | flops 50397184 | bytes 458752 | tf_op jit(solution)/shard_map/dot_general | solution.py:18
  (74 shorter events, 4.4 us)
Async XLA Ops:
  0.6 1.5 %copy-start.1 = (f32[32,256]{1,0:T(8,128)S(1)}, f32[32,256]{1,0:T(8,128)}, u32[]{:S(2)}) copy-start(f32[32,256]{1,0:T(8,128)} %param.9) | copy-start | bytes 98308
  2.1 7.3 %collective-permute-start = (f32[1,40,256]{2,1,0:T(8,128)S(1)}, f32[1,40,256]{2,1,0:T(8,128)S(1)}, u32[]{:S(2)}, u32[]{:S(2)}) collective-permute-start(f32[1,40,256]{2,1,0:T(8,128)S(1)} %fusion.18), channel_id=1, source_target_pairs={{0,8},{1,9},{2,10},{3,11},{4,12},{5,13},{6,14},{7,15},{8,0},{9,1},... | collective-permute-start | bytes 122888 | tf_op jit(solution)/shard_map/ppermute | solution.py:27
  5.2 5.7 %collective-permute-start.1 = (f32[1,40,256]{2,1,0:T(8,128)S(1)}, f32[1,40,256]{2,1,0:T(8,128)S(1)}, u32[]{:S(2)}, u32[]{:S(2)}) collective-permute-start(f32[1,40,256]{2,1,0:T(8,128)S(1)} %fusion.18), channel_id=1, source_target_pairs={{0,16},{1,17},{2,18},{3,19},{4,20},{5,21},{6,22},{7,23},{8,24},{9,... | collective-permute-start | bytes 122888 | tf_op jit(solution)/shard_map/ppermute | solution.py:27
  7.8 5.8 %collective-permute-start.2 = (f32[1,40,256]{2,1,0:T(8,128)S(1)}, f32[1,40,256]{2,1,0:T(8,128)S(1)}, u32[]{:S(2)}, u32[]{:S(2)}) collective-permute-start(f32[1,40,256]{2,1,0:T(8,128)S(1)} %fusion.18), channel_id=1, source_target_pairs={{0,24},{1,25},{2,26},{3,27},{4,28},{5,29},{6,30},{7,31},{8,16},{9,... | collective-permute-start | bytes 122888 | tf_op jit(solution)/shard_map/ppermute | solution.py:27
  8.0 1.1 %copy-start.2 = (f32[2,128]{1,0:T(2,128)S(1)}, f32[2,128]{1,0:T(2,128)}, u32[]{:S(2)}) copy-start(f32[2,128]{1,0:T(2,128)} %param.7) | copy-start | bytes 3076
  14.4 1.3 %collective-permute-start.3 = (f32[144,128]{1,0:T(8,128)S(1)}, f32[144,128]{1,0:T(8,128)S(1)}, u32[]{:S(2)}, u32[]{:S(2)}) collective-permute-start(f32[144,128]{1,0:T(8,128)S(1)} %pad_maximum_fusion.3), channel_id=1, source_target_pairs={{0,1},{1,0},{2,3},{3,2},{4,5},{5,4},{6,7},{7,6},{8,9},{9,8},{10,11... | collective-permute-start | bytes 221192 | tf_op jit(solution)/shard_map/ppermute | solution.py:27
  16.0 4.6 %collective-permute-start.4 = (f32[160,128]{1,0:T(8,128)S(1)}, f32[160,128]{1,0:T(8,128)S(1)}, u32[]{:S(2)}, u32[]{:S(2)}) collective-permute-start(f32[160,128]{1,0:T(8,128)S(1)} %pad_maximum_fusion.2), channel_id=1, source_target_pairs={{0,2},{1,3},{2,0},{3,1},{4,6},{5,7},{6,4},{7,5},{8,10},{9,11},{10,... | collective-permute-start | bytes 245768 | tf_op jit(solution)/shard_map/ppermute | solution.py:27
  17.6 5.3 %collective-permute-start.5 = (f32[160,128]{1,0:T(8,128)S(1)}, f32[160,128]{1,0:T(8,128)S(1)}, u32[]{:S(2)}, u32[]{:S(2)}) collective-permute-start(f32[160,128]{1,0:T(8,128)S(1)} %pad_maximum_fusion.2), channel_id=1, source_target_pairs={{0,4},{1,5},{2,6},{3,7},{4,0},{5,1},{6,2},{7,3},{8,12},{9,13},{10,... | collective-permute-start | bytes 245768 | tf_op jit(solution)/shard_map/ppermute | solution.py:27
  19.1 5.3 %collective-permute-start.6 = (f32[160,128]{1,0:T(8,128)S(1)}, f32[160,128]{1,0:T(8,128)S(1)}, u32[]{:S(2)}, u32[]{:S(2)}) collective-permute-start(f32[160,128]{1,0:T(8,128)S(1)} %pad_maximum_fusion.2), channel_id=1, source_target_pairs={{0,6},{1,7},{2,4},{3,5},{4,2},{5,3},{6,0},{7,1},{8,14},{9,15},{10,... | collective-permute-start | bytes 245768 | tf_op jit(solution)/shard_map/ppermute | solution.py:27
  24.4 4.8 %collective-permute-start.8 = (f32[128,128]{1,0:T(8,128)S(1)}, f32[128,128]{1,0:T(8,128)S(1)}, u32[]{:S(2)}, u32[]{:S(2)}) collective-permute-start(f32[128,128]{1,0:T(8,128)S(1)} %slice_add_fusion), channel_id=1, source_target_pairs={{0,1},{1,0},{2,3},{3,2},{4,5},{5,4},{6,7},{7,6},{8,9},{9,8},{10,11... | collective-permute-start | bytes 196616 | tf_op jit(solution)/shard_map/ppermute | solution.py:27
  24.5 5.4 %collective-permute-start.7 = (f32[128,128]{1,0:T(8,128)S(1)}, f32[128,128]{1,0:T(8,128)S(1)}, u32[]{:S(2)}, u32[]{:S(2)}) collective-permute-start(f32[128,128]{1,0:T(8,128)S(1)} %slice_add_fusion), channel_id=1, source_target_pairs={{0,24},{1,25},{2,16},{3,17},{4,8},{5,9},{6,0},{7,1},{8,10},{9,11},... | collective-permute-start | bytes 196616 | tf_op jit(solution)/shard_map/ppermute | solution.py:27
  29.6 1.2 %copy-start = (f32[256,128]{1,0:T(8,128)S(1)}, f32[256,128]{1,0:T(8,128)}, u32[]{:S(2)}) copy-start(f32[256,128]{1,0:T(8,128)} %param.11) | copy-start | bytes 393220

commit v3 on v2

--- a/solution.py
+++ b/solution.py
@@ -5,6 +5,8 @@
 
 length_scale = 0.3
 HIGHEST = lax.Precision.HIGHEST
+HIGH = lax.Precision.HIGH
+TWICE = True
 
 
 def matern(band_sites, test_sites):
@@ -14,8 +16,8 @@
     return (1.0 + scaled) * jnp.exp(-scaled)
 
 
-def dot(a, b, contract=((1,), (0,))):
-    return lax.dot_general(a, b, (contract, ((), ())), precision=HIGHEST, preferred_element_type=jnp.float32)
+def dot(a, b, contract=((1,), (0,)), precision=HIGHEST):
+    return lax.dot_general(a, b, (contract, ((), ())), precision=precision, preferred_element_type=jnp.float32)
 
 
 def permute(x, rows, cols, target):
@@ -49,7 +51,10 @@
 def gather(x, rows, cols, count, step):
     blocks = x[None]
     for stride, radix in stages(count):
-        blocks = jnp.concatenate([blocks] + [permute(blocks, rows, cols, step(d * stride)) for d in range(1, radix)])
+        got = []
+        for d in range(1, radix):
+            got.append(permute(blocks, rows, cols, step(d * stride)))
+        blocks = jnp.concatenate([blocks] + got)
     return blocks
 
 
@@ -57,18 +62,30 @@
     blocks, height = extra[None], x.shape[0]
     for stride, radix in stages(count):
         sent = jnp.concatenate([x, blocks.reshape(-1, x.shape[1])])
-        got = [permute(sent, rows, cols, step(d * stride)) for d in range(1, radix)]
+        got = []
+        for d in range(1, radix):
+            got.append(permute(sent, rows, cols, step(d * stride)))
         x = sum([g[:height] for g in got], x)
         blocks = jnp.concatenate([blocks] + [g[height:].reshape(blocks.shape) for g in got])
     return x, blocks
 
 
-def lower_inverse_t(u):
+def upper_inverse(u, base=16):
     size = u.shape[0]
     row = lax.broadcasted_iota(jnp.int32, u.shape, 0)
     col = lax.broadcasted_iota(jnp.int32, u.shape, 1)
-    inverse = jnp.where(row == col, 1.0 / u, 0.0)
-    block = 1
+    scale = jnp.sum(jnp.where(row == col, u, 0.0), axis=0, keepdims=True)
+    inside = (row // base == col // base) & (row < col)
+    power = jnp.where(inside, -u / scale, 0.0)
+    inverse = jnp.where(row == col, 1.0, power)
+    order = 2
+    while order < base:
+        power = dot(power, power)
+        inverse = inverse + dot(inverse, power)
+        order *= 2
+    down = jnp.sum(jnp.where(row == col, u, 0.0), axis=1, keepdims=True)
+    inverse = inverse / down
+    block = base
     while block < size:
         above = (row // (2 * block) == col // (2 * block)) & (row // block < col // block)
         inverse = inverse - dot(dot(inverse, jnp.where(above, u, 0.0)), inverse)
@@ -78,10 +95,10 @@
 
 def pack(prior_factor, band_factor, band_sites):
     width = prior_factor.shape[1]
-    turned = band_factor.T
-    parts = [turned[i : i + 8] for i in range(0, turned.shape[0], 8)]
-    parts.append(jnp.pad(band_sites, ((0, 8 - band_sites.shape[0]), (0, 0))))
-    low = jnp.concatenate(parts, axis=1)
+    tall = band_factor.shape[0]
+    sites = jnp.pad(band_sites, ((0, 8 - band_sites.shape[0]), (0, 0)))
+    low = jnp.concatenate([band_factor.T, sites])
+    low = low.reshape(-1, 8, tall).transpose(1, 0, 2).reshape(8, -1)
     low = jnp.pad(low, ((0, 0), (0, width - low.shape[1])))
     return jnp.concatenate([prior_factor, low])
 
@@ -119,24 +136,33 @@
     factor, turned, sites = unpack(blocks, tile_rows, tile_cols)
 
     halves = prior_solution.reshape(-1, 2, tile)
-    theirs = dot(factor, lax.dynamic_index_in_dim(halves, 1 - k, 1, keepdims=False))
-    mine = dot(factor, lax.dynamic_index_in_dim(halves, k, 1, keepdims=False))
+    theirs = dot(factor, lax.dynamic_index_in_dim(halves, 1 - k, 1, keepdims=False), precision=HIGH)
     turned = turned.reshape(-1, tile)
     got = permute(jnp.concatenate([theirs, turned]), rows, cols, other_core)
+    mine = dot(factor, lax.dynamic_index_in_dim(halves, k, 1, keepdims=False), precision=HIGH)
     cross = jnp.where(q == r, matern(sites, test_sites), 0.0)
-    part = (cross - mine) - got[:band]
+    mine = lax.optimization_barrier(cross - mine)
+    part = mine - got[:band]
     pair = natural(jnp.stack([turned, got[band:]]), k).reshape(-1, tile)
 
     rest, columns = reduce_and_gather(part, pair, rows, cols, cols // 2, along_col)
     moved = permute(rest, rows, cols, to_column)
     rest_other = permute(rest, rows, cols, other_core)
-    inverse = lower_inverse_t(natural(columns, q).reshape(band, band))
+    inverse = upper_inverse(natural(columns, q).reshape(band, band))
     first = ((0,), (0,))
-    both = natural(jnp.stack([dot(inverse, rest, first), dot(inverse, rest_other, first)]), k)
-    right = dot(inverse, jnp.where(q == r, rest, moved), first)
+    both = natural(jnp.stack([rest, rest_other]), k)
     left = jnp.concatenate([both[0], both[1]], axis=1)
-    band_solution = lax.dynamic_slice_in_dim(right, r * tile_rows, tile_rows, 0)
-    return band_solution, prior_covariance - dot(left, right, first)
+    if TWICE:
+        normal = dot(inverse, inverse, ((1,), (1,)))
+        left = dot(normal, left, precision=HIGH)
+        right = jnp.where(q == r, rest, moved)
+        own = lax.dynamic_slice_in_dim(inverse, r * tile_rows, tile_rows, 1)
+        band_solution = dot(own, right, first, HIGH)
+    else:
+        left = dot(inverse, left, first)
+        right = dot(inverse, jnp.where(q == r, rest, moved), first)
+        band_solution = lax.dynamic_slice_in_dim(right, r * tile_rows, tile_rows, 0)
+    return band_solution, prior_covariance - dot(left, right, first, HIGH)
 
 
 def solution(mesh):

time: 32 us -> 29.4 us (0.919)
  waiting for transfers between devices: 10.5 us -> 6.9 us
  starting transfers between devices: 10 us -> 11.1 us
    ppermute x9, waiting for transfers between devices: 10.5 us -> 6.9 us  [permute(): return lax.ppermute(x, ('row', 'col'), pairs)]
    unnamed x6 -> x8, local copies, waits for them, and re-layouts: 0.02 us -> 1.36 us
    ppermute x9, starting transfers between devices: 10 us -> 11.1 us  [permute(): return lax.ppermute(x, ('row', 'col'), pairs)]
    concatenate x2 -> x1, other arithmetic: 0.77 us -> 0.02 us  [gather(): blocks = jnp.concatenate([blocks] + got)]
    slice x1 -> x0, local copies, waits for them, and re-layouts: 0.71 us -> none  [pack(): parts = [turned[i:i + 8] for i in range(0, turned.shape[0], 8)]]
    reshape x0 -> x1, other arithmetic: none -> 0.71 us  [pack(): low = low.reshape(-1, 8, tall).transpose(1, 0, 2).reshape(8, -1)]
    dynamic_slice x2 -> x1, local copies, waits for them, and re-layouts: 0.85 us -> 0.23 us  [local(): lax.dynamic_index_in_dim(halves, k, 1, keepdims=False)]
    select_n x4 -> x2, other arithmetic: 0.77 us -> 0.41 us  [the longest x1 0.27 us: upper_inverse(): inverse = inverse - dot(dot(inverse, jnp.where(above, u, 0.0)), inverse)]
  transfers between devices with their start and end apart: 9 -> 9, of which waited for: 7 -> 5; matrix products, arithmetic and copies ran while one was open for 18% -> 19% of each run, Pallas kernels for 0% -> 0%
where the time goes in v3:
time: 29.4 us; the launch traced here: 29.1 us
  starting transfers between devices  11.1 us (38%)
  waiting for transfers between devices  6.9 us (23%)
  matrix products  5.18 us (18%)
  local copies, waits for them, and re-layouts  3.38 us (11%)
  other arithmetic  1.52 us (5%)
  between operations  1.04 us (4%)
    ppermute x9, starting transfers between devices, permute(): return lax.ppermute(x, ('row', 'col'), pairs)  11.1 us
    ppermute x9, waiting for transfers between devices, permute(): return lax.ppermute(x, ('row', 'col'), pairs)  6.9 us
    dot_general x18, matrix products, dot(): lax.dot_general(a, b, (contract, ((), ())), precision=precision, preferre...  5.18 us
    unnamed x8, local copies, waits for them, and re-layouts  1.36 us
    reshape x1, local copies, waits for them, and re-layouts, local(): halves = prior_solution.reshape(-1, 2, tile)  1.08 us
    reshape x1, other arithmetic, pack(): low = low.reshape(-1, 8, tall).transpose(1, 0, 2).reshape(8, -1)  0.71 us
  transfers between devices with their start and end apart: 9, of which 5 were waited for; matrix products, arithmetic and copies ran while one was open for 19% of the time, Pallas kernels for 0%

profile of v3, /device:TPU:0, one launch (start us, length us, event | category | flops | bytes accessed | tf_op | source)
XLA Modules:
  0.0 29.1 jit_solution(16678933475353096537)
XLA Ops:
  0.6 0.7 %copy-done.3 = f32[2,32]{1,0:T(2,128)S(1)} copy-done((f32[2,32]{1,0:T(2,128)S(1)}, f32[2,32]{1,0:T(2,128)}, u32[]{:S(2)}) %copy-start.3) | copy-done | bytes 280
  1.3 0.7 %fusion.23 = f32[3,8,32]{2,1,0:T(8,128)S(1)} fusion(f32[2,32]{1,0:T(2,128)S(1)} %copy-done.3, f32[16,32]{1,0:T(8,128)} %bitcast.105), kind=kLoop, calls=%fused_computation.75 | loop fusion | flops 2304 | bytes 5376 | tf_op jit(solution)/shard_map/reshape | solution.py:101
  2.1 5.1 %collective-permute-start.2 = (f32[1,40,256]{2,1,0:T(8,128)S(1)}, f32[1,40,256]{2,1,0:T(8,128)S(1)}, u32[]{:S(2)}, u32[]{:S(2)}) collective-permute-start(f32[1,40,256]{2,1,0:T(8,128)S(1)} %fusion.22), channel_id=1, source_target_pairs={{0,24},{1,25},{2,26},{3,27},{4,28},{5,29},{6,30},{7,31},{8,16},{9,... | collective-permute-start | bytes 122888 | tf_op jit(solution)/shard_map/ppermute | solution.py:29
  7.3 0.6 %collective-permute-start = (f32[1,40,256]{2,1,0:T(8,128)S(1)}, f32[1,40,256]{2,1,0:T(8,128)S(1)}, u32[]{:S(2)}, u32[]{:S(2)}) collective-permute-start(f32[1,40,256]{2,1,0:T(8,128)S(1)} %fusion.22), channel_id=1, source_target_pairs={{0,8},{1,9},{2,10},{3,11},{4,12},{5,13},{6,14},{7,15},{8,0},{9,1},... | collective-permute-start | bytes 122888 | tf_op jit(solution)/shard_map/ppermute | solution.py:29
  8.0 1.1 %reshape.241 = f32[256,2,128]{2,1,0:T(2,128)S(1)} reshape(f32[256,256]{1,0:T(8,128)} %param.10) | data formatting | bytes 524288 | tf_op jit(solution)/shard_map/reshape | solution.py:138
  9.1 0.7 %copy-done.2 = f32[2,128]{1,0:T(2,128)S(1)} copy-done((f32[2,128]{1,0:T(2,128)S(1)}, f32[2,128]{1,0:T(2,128)}, u32[]{:S(2)}) %copy-start.2) | copy-done | bytes 1048
  9.7 0.2 constant_dynamic-slice_fusion
  10.0 2.1 %collective-permute-done.1 = f32[1,40,256]{2,1,0:T(8,128)S(1)} collective-permute-done((f32[1,40,256]{2,1,0:T(8,128)S(1)}, f32[1,40,256]{2,1,0:T(8,128)S(1)}, u32[]{:S(2)}, u32[]{:S(2)}) %collective-permute-start.1) | collective-permute-done | bytes 40992 | tf_op jit(solution)/shard_map/ppermute | solution.py:29
  12.6 0.2 fusion.28
  13.1 0.2 convolution_subtract_fusion.4
  13.3 0.9 %collective-permute-done.3 = f32[144,128]{1,0:T(8,128)S(1)} collective-permute-done((f32[144,128]{1,0:T(8,128)S(1)}, f32[144,128]{1,0:T(8,128)S(1)}, u32[]{:S(2)}, u32[]{:S(2)}) %collective-permute-start.3) | collective-permute-done | bytes 73760 | tf_op jit(solution)/shard_map/ppermute | solution.py:29
  14.2 2.5 %collective-permute-start.6 = (f32[160,128]{1,0:T(8,128)S(1)}, f32[160,128]{1,0:T(8,128)S(1)}, u32[]{:S(2)}, u32[]{:S(2)}) collective-permute-start(f32[160,128]{1,0:T(8,128)S(1)} %pad_maximum_fusion.2), channel_id=1, source_target_pairs={{0,6},{1,7},{2,4},{3,5},{4,2},{5,3},{6,0},{7,1},{8,14},{9,15},{10,... | collective-permute-start | bytes 245768 | tf_op jit(solution)/shard_map/ppermute | solution.py:29
  16.7 0.5 %collective-permute-start.5 = (f32[160,128]{1,0:T(8,128)S(1)}, f32[160,128]{1,0:T(8,128)S(1)}, u32[]{:S(2)}, u32[]{:S(2)}) collective-permute-start(f32[160,128]{1,0:T(8,128)S(1)} %pad_maximum_fusion.2), channel_id=1, source_target_pairs={{0,4},{1,5},{2,6},{3,7},{4,0},{5,1},{6,2},{7,3},{8,12},{9,13},{10,... | collective-permute-start | bytes 245768 | tf_op jit(solution)/shard_map/ppermute | solution.py:29
  17.2 0.5 %collective-permute-start.4 = (f32[160,128]{1,0:T(8,128)S(1)}, f32[160,128]{1,0:T(8,128)S(1)}, u32[]{:S(2)}, u32[]{:S(2)}) collective-permute-start(f32[160,128]{1,0:T(8,128)S(1)} %pad_maximum_fusion.2), channel_id=1, source_target_pairs={{0,2},{1,3},{2,0},{3,1},{4,6},{5,7},{6,4},{7,5},{8,10},{9,11},{10,... | collective-permute-start | bytes 245768 | tf_op jit(solution)/shard_map/ppermute | solution.py:29
  17.8 2.0 %collective-permute-done.6 = f32[160,128]{1,0:T(8,128)S(1)} collective-permute-done((f32[160,128]{1,0:T(8,128)S(1)}, f32[160,128]{1,0:T(8,128)S(1)}, u32[]{:S(2)}, u32[]{:S(2)}) %collective-permute-start.6) | collective-permute-done | bytes 81952 | tf_op jit(solution)/shard_map/ppermute | solution.py:29
  19.7 1.7 %collective-permute-done.5 = f32[160,128]{1,0:T(8,128)S(1)} collective-permute-done((f32[160,128]{1,0:T(8,128)S(1)}, f32[160,128]{1,0:T(8,128)S(1)}, u32[]{:S(2)}, u32[]{:S(2)}) %collective-permute-start.5) | collective-permute-done | bytes 81952 | tf_op jit(solution)/shard_map/ppermute | solution.py:29
  21.4 0.2 collective-permute-done.4
  21.7 1.7 %collective-permute-start.7 = (f32[128,128]{1,0:T(8,128)S(1)}, f32[128,128]{1,0:T(8,128)S(1)}, u32[]{:S(2)}, u32[]{:S(2)}) collective-permute-start(f32[128,128]{1,0:T(8,128)S(1)} %slice_add_fusion), channel_id=1, source_target_pairs={{0,24},{1,25},{2,16},{3,17},{4,8},{5,9},{6,0},{7,1},{8,10},{9,11},... | collective-permute-start | bytes 196616 | tf_op jit(solution)/shard_map/ppermute | solution.py:29
  24.2 0.3 bitcast_select_fusion
  25.2 0.2 fusion
  26.5 0.2 convolution_subtract_fusion.1
  26.7 0.3 fusion.35
  27.3 0.9 %fusion.12 = f32[32,128]{1,0:T(8,128)} fusion(f32[128,128]{1,0:T(8,128)S(1)} %convolution_subtract_fusion.1, s32[]{:T(128)S(6)} %select_n.214, f32[128,128]{1,0:T(8,128)S(1)} %slice_add_fusion, f32[128,128]{1,0:T(8,128)S(1)} %collective-permute-done.7, pred[]{:T(512)S(6)} %eq.45), kind=kOutput, calls=%fused_computation.46 | convolution fusion | flops 3162112 | bytes 212997 | tf_op jit(solution)/shard_map/dot_general | solution.py:20
  28.2 0.9 %convolution_subtract_fusion = f32[256,128]{1,0:T(8,128)} fusion(f32[256,128]{1,0:T(8,128)S(1)} %copy-done, f32[128,256]{1,0:T(8,128)S(1)} %fusion.2, f32[128,128]{1,0:T(8,128)S(1)} %slice_add_fusion, f32[128,128]{1,0:T(8,128)S(1)} %collective-permute-done.7, pred[]{:T(512)S(6)} %eq.45), kind=kOutput, calls=%fused_computation | convolution fusion | flops 25214976 | bytes 524289 | tf_op jit(solution)/shard_map/dot_general | solution.py:20
  (70 shorter events, 3.6 us)
Async XLA Ops:
  0.6 0.7 %copy-start.3 = (f32[2,32]{1,0:T(2,128)S(1)}, f32[2,32]{1,0:T(2,128)}, u32[]{:S(2)}) copy-start(f32[2,32]{1,0:T(2,128)} %param.6) | copy-start | bytes 772
  1.3 0.8 %copy-start.1 = (f32[32,256]{1,0:T(8,128)S(1)}, f32[32,256]{1,0:T(8,128)}, u32[]{:S(2)}) copy-start(f32[32,256]{1,0:T(8,128)} %param.9) | copy-start | bytes 98308
  2.1 7.9 %collective-permute-start.2 = (f32[1,40,256]{2,1,0:T(8,128)S(1)}, f32[1,40,256]{2,1,0:T(8,128)S(1)}, u32[]{:S(2)}, u32[]{:S(2)}) collective-permute-start(f32[1,40,256]{2,1,0:T(8,128)S(1)} %fusion.22), channel_id=1, source_target_pairs={{0,24},{1,25},{2,26},{3,27},{4,28},{5,29},{6,30},{7,31},{8,16},{9,... | collective-permute-start | bytes 122888 | tf_op jit(solution)/shard_map/ppermute | solution.py:29
  7.3 4.9 %collective-permute-start.1 = (f32[1,40,256]{2,1,0:T(8,128)S(1)}, f32[1,40,256]{2,1,0:T(8,128)S(1)}, u32[]{:S(2)}, u32[]{:S(2)}) collective-permute-start(f32[1,40,256]{2,1,0:T(8,128)S(1)} %fusion.22), channel_id=1, source_target_pairs={{0,16},{1,17},{2,18},{3,19},{4,20},{5,21},{6,22},{7,23},{8,24},{9,... | collective-permute-start | bytes 122888 | tf_op jit(solution)/shard_map/ppermute | solution.py:29
  7.3 4.9 %collective-permute-start = (f32[1,40,256]{2,1,0:T(8,128)S(1)}, f32[1,40,256]{2,1,0:T(8,128)S(1)}, u32[]{:S(2)}, u32[]{:S(2)}) collective-permute-start(f32[1,40,256]{2,1,0:T(8,128)S(1)} %fusion.22), channel_id=1, source_target_pairs={{0,8},{1,9},{2,10},{3,11},{4,12},{5,13},{6,14},{7,15},{8,0},{9,1},... | collective-permute-start | bytes 122888 | tf_op jit(solution)/shard_map/ppermute | solution.py:29
  9.1 0.7 %copy-start.2 = (f32[2,128]{1,0:T(2,128)S(1)}, f32[2,128]{1,0:T(2,128)}, u32[]{:S(2)}) copy-start(f32[2,128]{1,0:T(2,128)} %param.7) | copy-start | bytes 3076
  12.8 1.3 %collective-permute-start.3 = (f32[144,128]{1,0:T(8,128)S(1)}, f32[144,128]{1,0:T(8,128)S(1)}, u32[]{:S(2)}, u32[]{:S(2)}) collective-permute-start(f32[144,128]{1,0:T(8,128)S(1)} %pad_maximum_fusion.3), channel_id=1, source_target_pairs={{0,1},{1,0},{2,3},{3,2},{4,5},{5,4},{6,7},{7,6},{8,9},{9,8},{10,11... | collective-permute-start | bytes 221192 | tf_op jit(solution)/shard_map/ppermute | solution.py:29
  14.2 5.5 %collective-permute-start.6 = (f32[160,128]{1,0:T(8,128)S(1)}, f32[160,128]{1,0:T(8,128)S(1)}, u32[]{:S(2)}, u32[]{:S(2)}) collective-permute-start(f32[160,128]{1,0:T(8,128)S(1)} %pad_maximum_fusion.2), channel_id=1, source_target_pairs={{0,6},{1,7},{2,4},{3,5},{4,2},{5,3},{6,0},{7,1},{8,14},{9,15},{10,... | collective-permute-start | bytes 245768 | tf_op jit(solution)/shard_map/ppermute | solution.py:29
  16.7 4.7 %collective-permute-start.5 = (f32[160,128]{1,0:T(8,128)S(1)}, f32[160,128]{1,0:T(8,128)S(1)}, u32[]{:S(2)}, u32[]{:S(2)}) collective-permute-start(f32[160,128]{1,0:T(8,128)S(1)} %pad_maximum_fusion.2), channel_id=1, source_target_pairs={{0,4},{1,5},{2,6},{3,7},{4,0},{5,1},{6,2},{7,3},{8,12},{9,13},{10,... | collective-permute-start | bytes 245768 | tf_op jit(solution)/shard_map/ppermute | solution.py:29
  17.2 4.4 %collective-permute-start.4 = (f32[160,128]{1,0:T(8,128)S(1)}, f32[160,128]{1,0:T(8,128)S(1)}, u32[]{:S(2)}, u32[]{:S(2)}) collective-permute-start(f32[160,128]{1,0:T(8,128)S(1)} %pad_maximum_fusion.2), channel_id=1, source_target_pairs={{0,2},{1,3},{2,0},{3,1},{4,6},{5,7},{6,4},{7,5},{8,10},{9,11},{10,... | collective-permute-start | bytes 245768 | tf_op jit(solution)/shard_map/ppermute | solution.py:29
  21.7 5.6 %collective-permute-start.7 = (f32[128,128]{1,0:T(8,128)S(1)}, f32[128,128]{1,0:T(8,128)S(1)}, u32[]{:S(2)}, u32[]{:S(2)}) collective-permute-start(f32[128,128]{1,0:T(8,128)S(1)} %slice_add_fusion), channel_id=1, source_target_pairs={{0,24},{1,25},{2,16},{3,17},{4,8},{5,9},{6,0},{7,1},{8,10},{9,11},... | collective-permute-start | bytes 196616 | tf_op jit(solution)/shard_map/ppermute | solution.py:29
  23.4 3.6 %collective-permute-start.8 = (f32[128,128]{1,0:T(8,128)S(1)}, f32[128,128]{1,0:T(8,128)S(1)}, u32[]{:S(2)}, u32[]{:S(2)}) collective-permute-start(f32[128,128]{1,0:T(8,128)S(1)} %slice_add_fusion), channel_id=1, source_target_pairs={{0,1},{1,0},{2,3},{3,2},{4,5},{5,4},{6,7},{7,6},{8,9},{9,8},{10,11... | collective-permute-start | bytes 196616 | tf_op jit(solution)/shard_map/ppermute | solution.py:29
  27.2 0.9 %copy-start = (f32[256,128]{1,0:T(8,128)S(1)}, f32[256,128]{1,0:T(8,128)}, u32[]{:S(2)}) copy-start(f32[256,128]{1,0:T(8,128)} %param.11) | copy-start | bytes 393220

commit v4 on v3

--- a/solution.py
+++ b/solution.py
@@ -1,12 +1,13 @@
 import jax
 import jax.numpy as jnp
 from jax import lax
+from jax.experimental import pallas as pl
+from jax.experimental.pallas import tpu as pltpu
 from jax.sharding import PartitionSpec as P
 
 length_scale = 0.3
 HIGHEST = lax.Precision.HIGHEST
 HIGH = lax.Precision.HIGH
-TWICE = True
 
 
 def matern(band_sites, test_sites):
@@ -36,6 +37,12 @@
         out.append((stride, radix))
         stride *= radix
     return out
+
+
+def matching(count, home, flip):
+    near = sorted(range(count), key=lambda chip: (bin(chip ^ home).count("1"), -chip if flip else chip))
+    far = sorted(range(count), key=lambda plane: -abs(plane - home))
+    return [plane for _, plane in sorted(zip(near, far))]
 
 
 def natural(blocks, index):
@@ -93,14 +100,106 @@
     return inverse
 
 
+def split(x):
+    high = x.astype(jnp.bfloat16)
+    return high, (x - high.astype(jnp.float32)).astype(jnp.bfloat16)
+
+
+def dot3(a, b):
+    one = lambda x, y: jnp.dot(x, y, preferred_element_type=jnp.float32)
+    return one(a[0], b[0]) + (one(a[0], b[1]) + one(a[1], b[0]))
+
+
+def fetch(x):
+    def body(x_ref, out_ref, sem):
+        copy = pltpu.make_async_copy(x_ref, out_ref, sem)
+        copy.start()
+        copy.wait()
+
+    return pl.pallas_call(
+        body,
+        out_shape=pltpu.VMEM(x.shape, x.dtype),
+        in_specs=[pl.BlockSpec(memory_space=pl.ANY)],
+        out_specs=pl.BlockSpec(memory_space=pltpu.VMEM),
+        scratch_shapes=[pltpu.SemaphoreType.DMA],
+        name="fetch",
+    )(x)
+
+
+def finish(own, left, right, prior_covariance):
+    tall, tile = prior_covariance.shape
+    pieces = 2
+    piece = tall // pieces
+
+    def body(own_ref, left_ref, right_ref, prior_ref, rows_ref, out_ref, rows_buf, buf, sems):
+        whole = split(right_ref[...])
+        rows_buf[...] = dot3(split(own_ref[...]), whole)
+        copies = [pltpu.make_async_copy(rows_buf, rows_ref, sems.at[pieces])]
+        copies[0].start()
+        for i in range(pieces):
+            part = pl.ds(i * piece, piece)
+            buf[part] = prior_ref[part] - dot3(split(left_ref[part]), whole)
+            copies.append(pltpu.make_async_copy(buf.at[part], out_ref.at[part], sems.at[i]))
+            copies[-1].start()
+        for copy in copies:
+            copy.wait()
+
+    vmem = pl.BlockSpec(memory_space=pltpu.VMEM)
+    hbm = pl.BlockSpec(memory_space=pl.ANY)
+    rows_shape = (own.shape[0], tile)
+    return pl.pallas_call(
+        body,
+        out_shape=(
+            jax.ShapeDtypeStruct(rows_shape, jnp.float32),
+            jax.ShapeDtypeStruct(prior_covariance.shape, jnp.float32),
+        ),
+        in_specs=[vmem] * 4,
+        out_specs=(hbm, hbm),
+        scratch_shapes=[
+            pltpu.VMEM(rows_shape, jnp.float32),
+            pltpu.VMEM(prior_covariance.shape, jnp.float32),
+            pltpu.SemaphoreType.DMA((pieces + 1,)),
+        ],
+        name="finish",
+    )(*[pltpu.with_memory_space_constraint(x, pltpu.VMEM) for x in (own, left, right, prior_covariance)])
+
+
 def pack(prior_factor, band_factor, band_sites):
-    width = prior_factor.shape[1]
-    tall = band_factor.shape[0]
-    sites = jnp.pad(band_sites, ((0, 8 - band_sites.shape[0]), (0, 0)))
-    low = jnp.concatenate([band_factor.T, sites])
-    low = low.reshape(-1, 8, tall).transpose(1, 0, 2).reshape(8, -1)
-    low = jnp.pad(low, ((0, 0), (0, width - low.shape[1])))
-    return jnp.concatenate([prior_factor, low])
+    height, width = prior_factor.shape
+    turned = band_factor.T
+    tall, wide = turned.shape
+    groups = tall // 8
+
+    def body(factor_ref, turned_ref, sites_ref, out_ref, turned_buf, sites_buf, sems):
+        copies = [
+            pltpu.make_async_copy(turned_ref, turned_buf, sems.at[0]),
+            pltpu.make_async_copy(sites_ref, sites_buf, sems.at[1]),
+            pltpu.make_async_copy(factor_ref, out_ref.at[pl.ds(0, height)], sems.at[2]),
+        ]
+        for copy in copies:
+            copy.start()
+        out_ref[height:, :] = jnp.zeros((8, width), jnp.float32)
+        copies[0].wait()
+        for i in range(groups):
+            out_ref[height:, i * wide : (i + 1) * wide] = turned_buf[8 * i : 8 * i + 8, :]
+        copies[1].wait()
+        count, span = sites_buf.shape
+        out_ref[height : height + count, groups * wide : groups * wide + span] = sites_buf[...]
+        copies[2].wait()
+
+    hbm = pl.BlockSpec(memory_space=pl.ANY)
+    return pl.pallas_call(
+        body,
+        out_shape=pltpu.VMEM((height + 8, width), jnp.float32),
+        in_specs=[hbm, hbm, hbm],
+        out_specs=pl.BlockSpec(memory_space=pltpu.VMEM),
+        scratch_shapes=[
+            pltpu.VMEM(turned.shape, jnp.float32),
+            pltpu.VMEM(band_sites.shape, jnp.float32),
+            pltpu.SemaphoreType.DMA((3,)),
+        ],
+        name="pack",
+    )(prior_factor, turned, band_sites)
 
 
 def unpack(blocks, tile_rows, tile_cols):
@@ -130,7 +229,7 @@
         return i, j ^ 1
 
     def to_column(i, j):
-        return (j // 2) ^ (rows - 1) ^ ((i + 1) & (rows // 2)), 2 * i + j % 2
+        return matching(rows, i, False)[j // 2], 2 * i + j % 2
 
     blocks = natural(gather(pack(prior_factor, band_factor, band_sites), rows, cols, rows, along_row), r)
     factor, turned, sites = unpack(blocks, tile_rows, tile_cols)
@@ -152,17 +251,11 @@
     first = ((0,), (0,))
     both = natural(jnp.stack([rest, rest_other]), k)
     left = jnp.concatenate([both[0], both[1]], axis=1)
-    if TWICE:
-        normal = dot(inverse, inverse, ((1,), (1,)))
-        left = dot(normal, left, precision=HIGH)
-        right = jnp.where(q == r, rest, moved)
-        own = lax.dynamic_slice_in_dim(inverse, r * tile_rows, tile_rows, 1)
-        band_solution = dot(own, right, first, HIGH)
-    else:
-        left = dot(inverse, left, first)
-        right = dot(inverse, jnp.where(q == r, rest, moved), first)
-        band_solution = lax.dynamic_slice_in_dim(right, r * tile_rows, tile_rows, 0)
-    return band_solution, prior_covariance - dot(left, right, first, HIGH)
+    prior = fetch(prior_covariance)
+    normal = dot(inverse, inverse, ((1,), (1,)))
+    left = dot(left, normal, first, HIGH)
+    own = lax.dynamic_slice_in_dim(inverse, r * tile_rows, tile_rows, 1).T
+    return finish(own, left, jnp.where(q == r, rest, moved), prior)
 
 
 def solution(mesh):

time: 29.4 us -> 29 us (0.986)
  Pallas kernels: 0 us -> 2.65 us
  matrix products: 5.18 us -> 3.42 us
  starting transfers between devices: 11.1 us -> 12.1 us
  waiting for transfers between devices: 6.9 us -> 5.97 us
  other arithmetic: 1.52 us -> 0.84 us
  local copies, waits for them, and re-layouts: 3.38 us -> 2.75 us
    pallas_call x0 -> x3, Pallas kernels: none -> 2.65 us  [the longest x1 0.92 us: fetch(): pl.pallas_call(body, out_shape=pltpu.VMEM(x.shape, x.dtype), in_specs=[pl...]
    dot_general x18 -> x16, matrix products: 5.18 us -> 3.42 us  [dot(): lax.dot_general(a, b, (contract, ((), ())), precision=precision, preferre...]
    ppermute x9, starting transfers between devices: 11.1 us -> 12.1 us  [permute(): return lax.ppermute(x, ('row', 'col'), pairs)]
    ppermute x9, waiting for transfers between devices: 6.9 us -> 5.97 us  [permute(): return lax.ppermute(x, ('row', 'col'), pairs)]
    reshape x1 -> x0, other arithmetic: 0.71 us -> none  [pack(): low = low.reshape(-1, 8, tall).transpose(1, 0, 2).reshape(8, -1)]
    unnamed x8 -> x2, local copies, waits for them, and re-layouts: 1.36 us -> 0.67 us
  transfers between devices with their start and end apart: 9 -> 9, of which waited for: 5 -> 5; matrix products, arithmetic and copies ran while one was open for 19% -> 20% of each run, Pallas kernels for 0% -> 3%
where the time goes in v4:
time: 29 us; the launch traced here: 28.8 us
  starting transfers between devices  12.1 us (42%)
  waiting for transfers between devices  5.97 us (21%)
  matrix products  3.42 us (12%)
  local copies, waits for them, and re-layouts  2.75 us (9%)
  Pallas kernels  2.65 us (9%)
  between operations  1.03 us (4%)
  other arithmetic  0.84 us (3%)
    ppermute x9, starting transfers between devices, permute(): return lax.ppermute(x, ('row', 'col'), pairs)  12.1 us
    ppermute x9, waiting for transfers between devices, permute(): return lax.ppermute(x, ('row', 'col'), pairs)  5.97 us
    dot_general x16, matrix products, dot(): lax.dot_general(a, b, (contract, ((), ())), precision=precision, preferre...  3.42 us
    reshape x1, local copies, waits for them, and re-layouts, local(): halves = prior_solution.reshape(-1, 2, tile)  1.08 us
    pallas_call x1, Pallas kernels, fetch(): pl.pallas_call(body, out_shape=pltpu.VMEM(x.shape, x.dtype), in_specs=[pl...  0.92 us
    pallas_call x1, Pallas kernels, finish(): pl.pallas_call(body, out_shape=(jax.ShapeDtypeStruct(rows_shape, jnp.floa...  0.88 us
    pallas_call x1, Pallas kernels, pack(): pl.pallas_call(body, out_shape=pltpu.VMEM((height + 8, width), jnp.float3...  0.86 us
    unnamed x2, local copies, waits for them, and re-layouts  0.67 us
  transfers between devices with their start and end apart: 9, of which 5 were waited for; matrix products, arithmetic and copies ran while one was open for 20% of the time, Pallas kernels for 3%

profile of v4, /device:TPU:0, one launch (start us, length us, event | category | flops | bytes accessed | tf_op | source)
XLA Modules:
  0.0 28.8 jit_solution(15840340261558090052)
XLA Ops:
  0.6 0.9 %pack.1 = f32[40,256]{1,0:T(8,128)S(1)} custom-call(f32[32,256]{1,0:T(8,128)} %factor_ref.1, f32[16,32]{1,0:T(8,128)} %bitcast.103, f32[2,32]{1,0:T(2,128)} %sites_ref.1), custom_call_target="tpu_custom_call" | custom-call | tf_op jit(solution)/shard_map/pack/pallas_call | solution.py:191
  1.5 5.1 %collective-permute-start.2 = (f32[1,40,256]{2,1,0:T(8,128)S(1)}, f32[1,40,256]{2,1,0:T(8,128)S(1)}, u32[]{:S(2)}, u32[]{:S(2)}) collective-permute-start(f32[1,40,256]{2,1,0:T(8,128)S(1)} %bitcast.86), channel_id=1, source_target_pairs={{0,24},{1,25},{2,26},{3,27},{4,28},{5,29},{6,30},{7,31},{8,16},{9,... | collective-permute-start | bytes 122888 | tf_op jit(solution)/shard_map/ppermute | solution.py:30
  6.6 0.6 %collective-permute-start = (f32[1,40,256]{2,1,0:T(8,128)S(1)}, f32[1,40,256]{2,1,0:T(8,128)S(1)}, u32[]{:S(2)}, u32[]{:S(2)}) collective-permute-start(f32[1,40,256]{2,1,0:T(8,128)S(1)} %bitcast.88), channel_id=1, source_target_pairs={{0,8},{1,9},{2,10},{3,11},{4,12},{5,13},{6,14},{7,15},{8,0},{9,1},... | collective-permute-start | bytes 122888 | tf_op jit(solution)/shard_map/ppermute | solution.py:30
  7.3 1.1 %reshape.233 = f32[256,2,128]{2,1,0:T(2,128)S(1)} reshape(f32[256,256]{1,0:T(8,128)} %param.10) | data formatting | bytes 524288 | tf_op jit(solution)/shard_map/reshape | solution.py:237
  8.5 0.7 %copy-done = f32[2,128]{1,0:T(2,128)S(1)} copy-done((f32[2,128]{1,0:T(2,128)S(1)}, f32[2,128]{1,0:T(2,128)}, u32[]{:S(2)}) %copy-start) | copy-done | bytes 1048
  9.1 0.2 constant_dynamic-slice_fusion
  9.4 0.9 %fetch.1.prior_ref = f32[256,128]{1,0:T(8,128)S(1)} custom-call(f32[256,128]{1,0:T(8,128)} %x_ref.1), custom_call_target="tpu_custom_call" | custom-call | tf_op jit(solution)/shard_map/fetch/pallas_call | solution.py:119
  10.3 1.2 %collective-permute-done.1 = f32[1,40,256]{2,1,0:T(8,128)S(1)} collective-permute-done((f32[1,40,256]{2,1,0:T(8,128)S(1)}, f32[1,40,256]{2,1,0:T(8,128)S(1)}, u32[]{:S(2)}, u32[]{:S(2)}) %collective-permute-start.1) | collective-permute-done | bytes 40992 | tf_op jit(solution)/shard_map/ppermute | solution.py:30
  12.0 0.2 fusion.23
  12.5 0.2 convolution_subtract_fusion.3
  12.7 0.9 %collective-permute-done.3 = f32[144,128]{1,0:T(8,128)S(1)} collective-permute-done((f32[144,128]{1,0:T(8,128)S(1)}, f32[144,128]{1,0:T(8,128)S(1)}, u32[]{:S(2)}, u32[]{:S(2)}) %collective-permute-start.3) | collective-permute-done | bytes 73760 | tf_op jit(solution)/shard_map/ppermute | solution.py:30
  13.6 2.5 %collective-permute-start.6 = (f32[160,128]{1,0:T(8,128)S(1)}, f32[160,128]{1,0:T(8,128)S(1)}, u32[]{:S(2)}, u32[]{:S(2)}) collective-permute-start(f32[160,128]{1,0:T(8,128)S(1)} %pad_maximum_fusion.2), channel_id=1, source_target_pairs={{0,6},{1,7},{2,4},{3,5},{4,2},{5,3},{6,0},{7,1},{8,14},{9,15},{10,... | collective-permute-start | bytes 245768 | tf_op jit(solution)/shard_map/ppermute | solution.py:30
  16.1 0.5 %collective-permute-start.5 = (f32[160,128]{1,0:T(8,128)S(1)}, f32[160,128]{1,0:T(8,128)S(1)}, u32[]{:S(2)}, u32[]{:S(2)}) collective-permute-start(f32[160,128]{1,0:T(8,128)S(1)} %pad_maximum_fusion.2), channel_id=1, source_target_pairs={{0,4},{1,5},{2,6},{3,7},{4,0},{5,1},{6,2},{7,3},{8,12},{9,13},{10,... | collective-permute-start | bytes 245768 | tf_op jit(solution)/shard_map/ppermute | solution.py:30
  16.6 0.5 %collective-permute-start.4 = (f32[160,128]{1,0:T(8,128)S(1)}, f32[160,128]{1,0:T(8,128)S(1)}, u32[]{:S(2)}, u32[]{:S(2)}) collective-permute-start(f32[160,128]{1,0:T(8,128)S(1)} %pad_maximum_fusion.2), channel_id=1, source_target_pairs={{0,2},{1,3},{2,0},{3,1},{4,6},{5,7},{6,4},{7,5},{8,10},{9,11},{10,... | collective-permute-start | bytes 245768 | tf_op jit(solution)/shard_map/ppermute | solution.py:30
  17.2 2.0 %collective-permute-done.6 = f32[160,128]{1,0:T(8,128)S(1)} collective-permute-done((f32[160,128]{1,0:T(8,128)S(1)}, f32[160,128]{1,0:T(8,128)S(1)}, u32[]{:S(2)}, u32[]{:S(2)}) %collective-permute-start.6) | collective-permute-done | bytes 81952 | tf_op jit(solution)/shard_map/ppermute | solution.py:30
  19.1 1.7 %collective-permute-done.5 = f32[160,128]{1,0:T(8,128)S(1)} collective-permute-done((f32[160,128]{1,0:T(8,128)S(1)}, f32[160,128]{1,0:T(8,128)S(1)}, u32[]{:S(2)}, u32[]{:S(2)}) %collective-permute-start.5) | collective-permute-done | bytes 81952 | tf_op jit(solution)/shard_map/ppermute | solution.py:30
  20.8 0.2 collective-permute-done.4
  21.2 2.6 %collective-permute-start.8 = (f32[128,128]{1,0:T(8,128)S(1)}, f32[128,128]{1,0:T(8,128)S(1)}, u32[]{:S(2)}, u32[]{:S(2)}) collective-permute-start(f32[128,128]{1,0:T(8,128)S(1)} %slice_add_fusion), channel_id=1, source_target_pairs={{0,24},{1,25},{2,16},{3,17},{4,8},{5,9},{6,0},{7,1},{8,2},{9,3},{1... | collective-permute-start | bytes 196616 | tf_op jit(solution)/shard_map/ppermute | solution.py:30
  24.6 0.3 bitcast_select_fusion
  25.6 0.2 fusion
  26.8 0.2 convolution_subtract_fusion
  27.0 0.3 fusion.30
  27.6 0.3 %fusion.2.left_ref = f32[256,128]{1,0:T(8,128)S(1)} fusion(f32[128,128]{1,0:T(8,128)S(1)} %fusion.30, f32[128,128]{1,0:T(8,128)S(1)} %slice_bitcast_fusion, f32[128,128]{1,0:T(8,128)S(1)} %slice_bitcast_fusion.1), kind=kOutput, calls=%fused_computation.14 | convolution fusion | flops 25198592 | bytes 327680 | tf_op jit(solution)/shard_map/dot_general | solution.py:21
  27.9 0.9 %finish.1 = (f32[32,128]{1,0:T(8,128)}, f32[256,128]{1,0:T(8,128)}) custom-call(f32[32,128]{1,0:T(8,128)S(1)} %copy.26.own_ref, f32[256,128]{1,0:T(8,128)S(1)} %fusion.2.left_ref, f32[128,128]{1,0:T(8,128)S(1)} %broadcast_select_fusion.right_ref, f32[256,128]{1,0:T(8,128)S(1)} %fetch.1.prior_ref), custom_call_target="tpu_custom_call" | custom-call | tf_op jit(solution)/shard_map/finish/pallas_call | solution.py:150
  (64 shorter events, 3.5 us)
Async XLA Ops:
  1.5 8.8 %collective-permute-start.2 = (f32[1,40,256]{2,1,0:T(8,128)S(1)}, f32[1,40,256]{2,1,0:T(8,128)S(1)}, u32[]{:S(2)}, u32[]{:S(2)}) collective-permute-start(f32[1,40,256]{2,1,0:T(8,128)S(1)} %bitcast.86), channel_id=1, source_target_pairs={{0,24},{1,25},{2,26},{3,27},{4,28},{5,29},{6,30},{7,31},{8,16},{9,... | collective-permute-start | bytes 122888 | tf_op jit(solution)/shard_map/ppermute | solution.py:30
  6.6 4.9 %collective-permute-start.1 = (f32[1,40,256]{2,1,0:T(8,128)S(1)}, f32[1,40,256]{2,1,0:T(8,128)S(1)}, u32[]{:S(2)}, u32[]{:S(2)}) collective-permute-start(f32[1,40,256]{2,1,0:T(8,128)S(1)} %bitcast.87), channel_id=1, source_target_pairs={{0,16},{1,17},{2,18},{3,19},{4,20},{5,21},{6,22},{7,23},{8,24},{9,... | collective-permute-start | bytes 122888 | tf_op jit(solution)/shard_map/ppermute | solution.py:30
  6.6 4.9 %collective-permute-start = (f32[1,40,256]{2,1,0:T(8,128)S(1)}, f32[1,40,256]{2,1,0:T(8,128)S(1)}, u32[]{:S(2)}, u32[]{:S(2)}) collective-permute-start(f32[1,40,256]{2,1,0:T(8,128)S(1)} %bitcast.88), channel_id=1, source_target_pairs={{0,8},{1,9},{2,10},{3,11},{4,12},{5,13},{6,14},{7,15},{8,0},{9,1},... | collective-permute-start | bytes 122888 | tf_op jit(solution)/shard_map/ppermute | solution.py:30
  8.4 0.7 %copy-start = (f32[2,128]{1,0:T(2,128)S(1)}, f32[2,128]{1,0:T(2,128)}, u32[]{:S(2)}) copy-start(f32[2,128]{1,0:T(2,128)} %param.7) | copy-start | bytes 3076
  12.2 1.3 %collective-permute-start.3 = (f32[144,128]{1,0:T(8,128)S(1)}, f32[144,128]{1,0:T(8,128)S(1)}, u32[]{:S(2)}, u32[]{:S(2)}) collective-permute-start(f32[144,128]{1,0:T(8,128)S(1)} %pad_maximum_fusion.3), channel_id=1, source_target_pairs={{0,1},{1,0},{2,3},{3,2},{4,5},{5,4},{6,7},{7,6},{8,9},{9,8},{10,11... | collective-permute-start | bytes 221192 | tf_op jit(solution)/shard_map/ppermute | solution.py:30
  13.6 5.5 %collective-permute-start.6 = (f32[160,128]{1,0:T(8,128)S(1)}, f32[160,128]{1,0:T(8,128)S(1)}, u32[]{:S(2)}, u32[]{:S(2)}) collective-permute-start(f32[160,128]{1,0:T(8,128)S(1)} %pad_maximum_fusion.2), channel_id=1, source_target_pairs={{0,6},{1,7},{2,4},{3,5},{4,2},{5,3},{6,0},{7,1},{8,14},{9,15},{10,... | collective-permute-start | bytes 245768 | tf_op jit(solution)/shard_map/ppermute | solution.py:30
  16.1 4.7 %collective-permute-start.5 = (f32[160,128]{1,0:T(8,128)S(1)}, f32[160,128]{1,0:T(8,128)S(1)}, u32[]{:S(2)}, u32[]{:S(2)}) collective-permute-start(f32[160,128]{1,0:T(8,128)S(1)} %pad_maximum_fusion.2), channel_id=1, source_target_pairs={{0,4},{1,5},{2,6},{3,7},{4,0},{5,1},{6,2},{7,3},{8,12},{9,13},{10,... | collective-permute-start | bytes 245768 | tf_op jit(solution)/shard_map/ppermute | solution.py:30
  16.6 4.4 %collective-permute-start.4 = (f32[160,128]{1,0:T(8,128)S(1)}, f32[160,128]{1,0:T(8,128)S(1)}, u32[]{:S(2)}, u32[]{:S(2)}) collective-permute-start(f32[160,128]{1,0:T(8,128)S(1)} %pad_maximum_fusion.2), channel_id=1, source_target_pairs={{0,2},{1,3},{2,0},{3,1},{4,6},{5,7},{6,4},{7,5},{8,10},{9,11},{10,... | collective-permute-start | bytes 245768 | tf_op jit(solution)/shard_map/ppermute | solution.py:30
  21.1 6.4 %collective-permute-start.7 = (f32[128,128]{1,0:T(8,128)S(1)}, f32[128,128]{1,0:T(8,128)S(1)}, u32[]{:S(2)}, u32[]{:S(2)}) collective-permute-start(f32[128,128]{1,0:T(8,128)S(1)} %slice_add_fusion), channel_id=1, source_target_pairs={{0,1},{1,0},{2,3},{3,2},{4,5},{5,4},{6,7},{7,6},{8,9},{9,8},{10,11... | collective-permute-start | bytes 196616 | tf_op jit(solution)/shard_map/ppermute | solution.py:30
  21.2 6.7 %collective-permute-start.8 = (f32[128,128]{1,0:T(8,128)S(1)}, f32[128,128]{1,0:T(8,128)S(1)}, u32[]{:S(2)}, u32[]{:S(2)}) collective-permute-start(f32[128,128]{1,0:T(8,128)S(1)} %slice_add_fusion), channel_id=1, source_target_pairs={{0,24},{1,25},{2,16},{3,17},{4,8},{5,9},{6,0},{7,1},{8,2},{9,3},{1... | collective-permute-start | bytes 196616 | tf_op jit(solution)/shard_map/ppermute | solution.py:30

commit v5 on v4

--- a/solution.py
+++ b/solution.py
@@ -77,7 +77,7 @@
     return x, blocks
 
 
-def upper_inverse(u, base=16):
+def upper_inverse(u, product, base=16):
     size = u.shape[0]
     row = lax.broadcasted_iota(jnp.int32, u.shape, 0)
     col = lax.broadcasted_iota(jnp.int32, u.shape, 1)
@@ -87,15 +87,15 @@
     inverse = jnp.where(row == col, 1.0, power)
     order = 2
     while order < base:
-        power = dot(power, power)
-        inverse = inverse + dot(inverse, power)
+        power = product(power, power)
+        inverse = inverse + product(inverse, power)
         order *= 2
     down = jnp.sum(jnp.where(row == col, u, 0.0), axis=1, keepdims=True)
     inverse = inverse / down
     block = base
     while block < size:
         above = (row // (2 * block) == col // (2 * block)) & (row // block < col // block)
-        inverse = inverse - dot(dot(inverse, jnp.where(above, u, 0.0)), inverse)
+        inverse = inverse - product(product(inverse, jnp.where(above, u, 0.0)), inverse)
         block *= 2
     return inverse
 
@@ -108,6 +108,32 @@
 def dot3(a, b):
     one = lambda x, y: jnp.dot(x, y, preferred_element_type=jnp.float32)
     return one(a[0], b[0]) + (one(a[0], b[1]) + one(a[1], b[0]))
+
+
+def invert(u, tile_rows):
+    size = u.shape[0]
+
+    def body(u_ref, own_ref, normal_ref, turned_buf):
+        inverse = upper_inverse(u_ref[...], product3)
+        turned = inverse.T
+        turned_buf[...] = turned
+        start = pl.multiple_of(lax.axis_index("row") * tile_rows, 8)
+        own_ref[...] = turned_buf[pl.ds(start, tile_rows)]
+        normal_ref[...] = product3(inverse, turned)
+
+    vmem = pl.BlockSpec(memory_space=pltpu.VMEM)
+    return pl.pallas_call(
+        body,
+        out_shape=(pltpu.VMEM((tile_rows, size), jnp.float32), pltpu.VMEM(u.shape, jnp.float32)),
+        in_specs=[vmem],
+        out_specs=(vmem, vmem),
+        scratch_shapes=[pltpu.VMEM(u.shape, jnp.float32)],
+        name="invert",
+    )(pltpu.with_memory_space_constraint(u, pltpu.VMEM))
+
+
+def product3(a, b):
+    return dot3(split(a), split(b))
 
 
 def fetch(x):
@@ -124,6 +150,66 @@
         scratch_shapes=[pltpu.SemaphoreType.DMA],
         name="fetch",
     )(x)
+
+
+def fetch_halves(x, tile):
+    shape = (x.shape[0], tile)
+
+    def body(x_ref, mine_ref, theirs_ref, sems):
+        k = lax.axis_index("col") % 2
+        columns = lambda half: x_ref.at[:, pl.ds(pl.multiple_of(half * tile, 128), tile)]
+        copies = [
+            pltpu.make_async_copy(columns(1 - k), theirs_ref, sems.at[0]),
+            pltpu.make_async_copy(columns(k), mine_ref, sems.at[1]),
+        ]
+        for copy in copies:
+            copy.start()
+        for copy in copies:
+            copy.wait()
+
+    vmem = pl.BlockSpec(memory_space=pltpu.VMEM)
+    return pl.pallas_call(
+        body,
+        out_shape=(pltpu.VMEM(shape, x.dtype), pltpu.VMEM(shape, x.dtype)),
+        in_specs=[pl.BlockSpec(memory_space=pl.ANY)],
+        out_specs=(vmem, vmem),
+        scratch_shapes=[pltpu.SemaphoreType.DMA((2,))],
+        name="fetch_halves",
+    )(x)
+
+
+def first_product(blocks, theirs, tile_rows, tile_cols):
+    count, _, width = blocks.shape
+    band, tile = count * tile_rows, theirs.shape[1]
+    groups = tile_cols // 8
+
+    def body(blocks_ref, theirs_ref, factor_ref, product_ref, turned_ref, sites_ref):
+        r = lax.axis_index("row")
+        for j in range(count):
+            start = pl.multiple_of((r ^ j) * tile_rows, 8)
+            factor_ref[pl.ds(start, tile_rows)] = blocks_ref[j, :tile_rows]
+        product_ref[...] = product3(factor_ref[...], theirs_ref[...])
+        for g in range(groups + 1):
+            pieces = [blocks_ref[j, tile_rows:, g * tile_rows : (g + 1) * tile_rows] for j in range(count)]
+            bit = 1
+            while bit < count:
+                pieces = [jnp.where((r & bit) != 0, pieces[j ^ bit], pieces[j]) for j in range(count)]
+                bit *= 2
+            row = jnp.concatenate(pieces, axis=1)
+            if g < groups:
+                turned_ref[8 * g : 8 * g + 8] = row
+            else:
+                sites_ref[...] = row
+
+    vmem = pl.BlockSpec(memory_space=pltpu.VMEM)
+    here = lambda *shape: pltpu.VMEM(shape, jnp.float32)
+    return pl.pallas_call(
+        body,
+        out_shape=(here(band, width), here(band, tile), here(tile_cols, band), here(8, band)),
+        in_specs=[vmem, vmem],
+        out_specs=(vmem,) * 4,
+        name="first_product",
+    )(*[pltpu.with_memory_space_constraint(x, pltpu.VMEM) for x in (blocks, theirs)])
 
 
 def finish(own, left, right, prior_covariance):
@@ -202,15 +288,6 @@
     )(prior_factor, turned, band_sites)
 
 
-def unpack(blocks, tile_rows, tile_cols):
-    factor = blocks[:, :tile_rows].reshape(-1, blocks.shape[2])
-    low = blocks[:, tile_rows:].transpose(1, 0, 2)
-    lanes = lambda i: low[:, :, i * tile_rows : (i + 1) * tile_rows].reshape(8, -1)
-    groups = tile_cols // 8
-    turned = jnp.concatenate([lanes(i) for i in range(groups)])
-    return factor, turned, lanes(groups)[:2]
-
-
 def local(band_sites, test_sites, band_factor, prior_factor, prior_solution, prior_covariance):
     rows, cols = lax.axis_size("row"), lax.axis_size("col")
     tile = test_sites.shape[1]
@@ -231,14 +308,12 @@
     def to_column(i, j):
         return matching(rows, i, False)[j // 2], 2 * i + j % 2
 
-    blocks = natural(gather(pack(prior_factor, band_factor, band_sites), rows, cols, rows, along_row), r)
-    factor, turned, sites = unpack(blocks, tile_rows, tile_cols)
-
-    halves = prior_solution.reshape(-1, 2, tile)
-    theirs = dot(factor, lax.dynamic_index_in_dim(halves, 1 - k, 1, keepdims=False), precision=HIGH)
+    half, other_half = fetch_halves(prior_solution, tile)
+    blocks = gather(pack(prior_factor, band_factor, band_sites), rows, cols, rows, along_row)
+    factor, theirs, turned, sites = first_product(blocks, other_half, tile_rows, tile_cols)
     turned = turned.reshape(-1, tile)
     got = permute(jnp.concatenate([theirs, turned]), rows, cols, other_core)
-    mine = dot(factor, lax.dynamic_index_in_dim(halves, k, 1, keepdims=False), precision=HIGH)
+    mine = dot(factor, half, precision=HIGH)
     cross = jnp.where(q == r, matern(sites, test_sites), 0.0)
     mine = lax.optimization_barrier(cross - mine)
     part = mine - got[:band]
@@ -247,14 +322,18 @@
     rest, columns = reduce_and_gather(part, pair, rows, cols, cols // 2, along_col)
     moved = permute(rest, rows, cols, to_column)
     rest_other = permute(rest, rows, cols, other_core)
-    inverse = upper_inverse(natural(columns, q).reshape(band, band))
+    triangle = natural(columns, q).reshape(band, band)
+    if band <= 256:
+        own, normal = invert(triangle, tile_rows)
+    else:
+        inverse = upper_inverse(triangle, dot)
+        normal = dot(inverse, inverse, ((1,), (1,)))
+        own = lax.dynamic_slice_in_dim(inverse, r * tile_rows, tile_rows, 1).T
     first = ((0,), (0,))
     both = natural(jnp.stack([rest, rest_other]), k)
     left = jnp.concatenate([both[0], both[1]], axis=1)
     prior = fetch(prior_covariance)
-    normal = dot(inverse, inverse, ((1,), (1,)))
     left = dot(left, normal, first, HIGH)
-    own = lax.dynamic_slice_in_dim(inverse, r * tile_rows, tile_rows, 1).T
     return finish(own, left, jnp.where(q == r, rest, moved), prior)
 
 

time: 29 us -> 27.2 us (0.938)
  Pallas kernels: 2.65 us -> 5.8 us
  matrix products: 3.42 us -> 0.5 us
  local copies, waits for them, and re-layouts: 2.75 us -> 0.04 us
  waiting for transfers between devices: 5.97 us -> 8.61 us
  starting transfers between devices: 12.1 us -> 11.1 us
  other arithmetic: 0.84 us -> 0.15 us
    pallas_call x0 -> x3, Pallas kernels: none -> 3.14 us  [the longest x1 1.95 us: invert(): pl.pallas_call(body, out_shape=(pltpu.VMEM((tile_rows, size), jnp.float32...]
    dot_general x16 -> x2, matrix products: 3.42 us -> 0.5 us  [dot(): lax.dot_general(a, b, (contract, ((), ())), precision=precision, preferre...]
    ppermute x9, waiting for transfers between devices: 5.97 us -> 8.61 us  [permute(): return lax.ppermute(x, ('row', 'col'), pairs)]
    reshape x3 -> x0, local copies, waits for them, and re-layouts: 1.25 us -> none  [the longest x1 1.08 us: local(): halves = prior_solution.reshape(-1, 2, tile)]
    ppermute x9, starting transfers between devices: 12.1 us -> 11.1 us  [permute(): return lax.ppermute(x, ('row', 'col'), pairs)]
    unnamed x2, local copies, waits for them, and re-layouts: 0.67 us -> 0.01 us
    select_n x2 -> x0, other arithmetic: 0.41 us -> none  [the longest x1 0.27 us: upper_inverse(): inverse = inverse - dot(dot(inverse, jnp.where(above, u, 0.0)), inverse)]
  transfers between devices with their start and end apart: 9 -> 9, of which waited for: 5 -> 7; matrix products, arithmetic and copies ran while one was open for 20% -> 2% of each run, Pallas kernels for 3% -> 14%
where the time goes in v5:
time: 27.2 us; the launch traced here: 27 us
  starting transfers between devices  11.1 us (41%)
  waiting for transfers between devices  8.61 us (32%)
  Pallas kernels  5.8 us (21%)
  between operations  0.84 us (3%)
  matrix products  0.5 us (2%)
    ppermute x9, starting transfers between devices, permute(): return lax.ppermute(x, ('row', 'col'), pairs)  11.1 us
    ppermute x9, waiting for transfers between devices, permute(): return lax.ppermute(x, ('row', 'col'), pairs)  8.61 us
    pallas_call x1, Pallas kernels, invert(): pl.pallas_call(body, out_shape=(pltpu.VMEM((tile_rows, size), jnp.float32...  1.95 us
    pallas_call x1, Pallas kernels, fetch_halves(): pl.pallas_call(body, out_shape=(pltpu.VMEM(shape, x.dtype), pltpu.VMEM(sh...  0.98 us
    pallas_call x1, Pallas kernels, fetch(): pl.pallas_call(body, out_shape=pltpu.VMEM(x.shape, x.dtype), in_specs=[pl...  0.91 us
    pallas_call x1, Pallas kernels, finish(): pl.pallas_call(body, out_shape=(jax.ShapeDtypeStruct(rows_shape, jnp.floa...  0.88 us
    pallas_call x1, Pallas kernels, pack(): pl.pallas_call(body, out_shape=pltpu.VMEM((height + 8, width), jnp.float3...  0.86 us
  transfers between devices with their start and end apart: 9, of which 7 were waited for; matrix products, arithmetic and copies ran while one was open for 2% of the time, Pallas kernels for 14%

profile of v5, /device:TPU:0, one launch (start us, length us, event | category | flops | bytes accessed | tf_op | source)
XLA Modules:
  0.0 27.0 jit_solution(9298920427928598117)
XLA Ops:
  0.6 0.9 %pack.1 = f32[40,256]{1,0:T(8,128)S(1)} custom-call(f32[32,256]{1,0:T(8,128)} %factor_ref.1, f32[16,32]{1,0:T(8,128)} %bitcast.50, f32[2,32]{1,0:T(2,128)} %sites_ref.1), custom_call_target="tpu_custom_call" | custom-call | tf_op jit(solution)/shard_map/pack/pallas_call | solution.py:277
  1.5 0.0 copy-start
  1.5 5.1 %collective-permute-start.2 = (f32[1,40,256]{2,1,0:T(8,128)S(1)}, f32[1,40,256]{2,1,0:T(8,128)S(1)}, u32[]{:S(2)}, u32[]{:S(2)}) collective-permute-start(f32[1,40,256]{2,1,0:T(8,128)S(1)} %bitcast.40), channel_id=1, source_target_pairs={{0,24},{1,25},{2,26},{3,27},{4,28},{5,29},{6,30},{7,31},{8,16},{9,... | collective-permute-start | bytes 122888 | tf_op jit(solution)/shard_map/ppermute | solution.py:30
  6.7 0.6 %collective-permute-start = (f32[1,40,256]{2,1,0:T(8,128)S(1)}, f32[1,40,256]{2,1,0:T(8,128)S(1)}, u32[]{:S(2)}, u32[]{:S(2)}) collective-permute-start(f32[1,40,256]{2,1,0:T(8,128)S(1)} %bitcast.42), channel_id=1, source_target_pairs={{0,8},{1,9},{2,10},{3,11},{4,12},{5,13},{6,14},{7,15},{8,0},{9,1},... | collective-permute-start | bytes 122888 | tf_op jit(solution)/shard_map/ppermute | solution.py:30
  7.3 1.0 %fetch_halves.1 = (f32[256,128]{1,0:T(8,128)S(1)}, f32[256,128]{1,0:T(8,128)S(1)}) custom-call(f32[256,256]{1,0:T(8,128)} %x_ref.2), custom_call_target="tpu_custom_call" | custom-call | tf_op jit(solution)/shard_map/fetch_halves/pallas_call | solution.py:171
  8.3 0.3 %collective-permute-done.2 = f32[1,40,256]{2,1,0:T(8,128)S(1)} collective-permute-done((f32[1,40,256]{2,1,0:T(8,128)S(1)}, f32[1,40,256]{2,1,0:T(8,128)S(1)}, u32[]{:S(2)}, u32[]{:S(2)}) %collective-permute-start.2) | collective-permute-done | bytes 40992 | tf_op jit(solution)/shard_map/ppermute | solution.py:30
  8.6 2.9 %collective-permute-done.1 = f32[1,40,256]{2,1,0:T(8,128)S(1)} collective-permute-done((f32[1,40,256]{2,1,0:T(8,128)S(1)}, f32[1,40,256]{2,1,0:T(8,128)S(1)}, u32[]{:S(2)}, u32[]{:S(2)}) %collective-permute-start.1) | collective-permute-done | bytes 40992 | tf_op jit(solution)/shard_map/ppermute | solution.py:30
  11.6 0.2 first_product.1
  11.8 0.1 collective-permute-start.3
  11.9 0.2 convolution_subtract_fusion
  12.1 1.0 %collective-permute-done.3 = f32[144,128]{1,0:T(8,128)S(1)} collective-permute-done((f32[144,128]{1,0:T(8,128)S(1)}, f32[144,128]{1,0:T(8,128)S(1)}, u32[]{:S(2)}, u32[]{:S(2)}) %collective-permute-start.3) | collective-permute-done | bytes 73760 | tf_op jit(solution)/shard_map/ppermute | solution.py:30
  13.2 2.5 %collective-permute-start.6 = (f32[160,128]{1,0:T(8,128)S(1)}, f32[160,128]{1,0:T(8,128)S(1)}, u32[]{:S(2)}, u32[]{:S(2)}) collective-permute-start(f32[160,128]{1,0:T(8,128)S(1)} %pad_maximum_fusion.2), channel_id=1, source_target_pairs={{0,6},{1,7},{2,4},{3,5},{4,2},{5,3},{6,0},{7,1},{8,14},{9,15},{10,... | collective-permute-start | bytes 245768 | tf_op jit(solution)/shard_map/ppermute | solution.py:30
  15.7 0.5 %collective-permute-start.5 = (f32[160,128]{1,0:T(8,128)S(1)}, f32[160,128]{1,0:T(8,128)S(1)}, u32[]{:S(2)}, u32[]{:S(2)}) collective-permute-start(f32[160,128]{1,0:T(8,128)S(1)} %pad_maximum_fusion.2), channel_id=1, source_target_pairs={{0,4},{1,5},{2,6},{3,7},{4,0},{5,1},{6,2},{7,3},{8,12},{9,13},{10,... | collective-permute-start | bytes 245768 | tf_op jit(solution)/shard_map/ppermute | solution.py:30
  16.2 0.5 %collective-permute-start.4 = (f32[160,128]{1,0:T(8,128)S(1)}, f32[160,128]{1,0:T(8,128)S(1)}, u32[]{:S(2)}, u32[]{:S(2)}) collective-permute-start(f32[160,128]{1,0:T(8,128)S(1)} %pad_maximum_fusion.2), channel_id=1, source_target_pairs={{0,2},{1,3},{2,0},{3,1},{4,6},{5,7},{6,4},{7,5},{8,10},{9,11},{10,... | collective-permute-start | bytes 245768 | tf_op jit(solution)/shard_map/ppermute | solution.py:30
  16.7 0.9 %fetch.1.prior_ref = f32[256,128]{1,0:T(8,128)S(1)} custom-call(f32[256,128]{1,0:T(8,128)} %x_ref.3), custom_call_target="tpu_custom_call" | custom-call | tf_op jit(solution)/shard_map/fetch/pallas_call | solution.py:145
  17.7 1.0 %collective-permute-done.6 = f32[160,128]{1,0:T(8,128)S(1)} collective-permute-done((f32[160,128]{1,0:T(8,128)S(1)}, f32[160,128]{1,0:T(8,128)S(1)}, u32[]{:S(2)}, u32[]{:S(2)}) %collective-permute-start.6) | collective-permute-done | bytes 81952 | tf_op jit(solution)/shard_map/ppermute | solution.py:30
  18.7 1.7 %collective-permute-done.5 = f32[160,128]{1,0:T(8,128)S(1)} collective-permute-done((f32[160,128]{1,0:T(8,128)S(1)}, f32[160,128]{1,0:T(8,128)S(1)}, u32[]{:S(2)}, u32[]{:S(2)}) %collective-permute-start.5) | collective-permute-done | bytes 81952 | tf_op jit(solution)/shard_map/ppermute | solution.py:30
  20.4 0.2 collective-permute-done.4
  20.7 0.1 collective-permute-start.7
  20.7 1.6 %collective-permute-start.8 = (f32[128,128]{1,0:T(8,128)S(1)}, f32[128,128]{1,0:T(8,128)S(1)}, u32[]{:S(2)}, u32[]{:S(2)}) collective-permute-start(f32[128,128]{1,0:T(8,128)S(1)} %slice_add_fusion), channel_id=1, source_target_pairs={{0,24},{1,25},{2,16},{3,17},{4,8},{5,9},{6,0},{7,1},{8,2},{9,3},{1... | collective-permute-start | bytes 196616 | tf_op jit(solution)/shard_map/ppermute | solution.py:30
  22.4 1.9 %invert.1 = (f32[32,128]{1,0:T(8,128)S(1)}, f32[128,128]{1,0:T(8,128)S(1)}) custom-call(f32[128,128]{1,0:T(8,128)S(1)} %bitcast.39), custom_call_target="tpu_custom_call" | custom-call | tf_op jit(solution)/shard_map/invert/pallas_call | solution.py:125
  24.5 0.3 %fusion.left_ref = f32[256,128]{1,0:T(8,128)S(1)} fusion(f32[128,128]{1,0:T(8,128)S(1)} %get-tuple-element.17, f32[128,128]{1,0:T(8,128)S(1)} %slice_bitcast_fusion, f32[128,128]{1,0:T(8,128)S(1)} %slice_bitcast_fusion.1), kind=kOutput, calls=%fused_computation.4 | convolution fusion | flops 25198592 | bytes 327680 | tf_op jit(solution)/shard_map/dot_general | solution.py:21
  24.8 1.4 %collective-permute-done.8 = f32[128,128]{1,0:T(8,128)S(1)} collective-permute-done((f32[128,128]{1,0:T(8,128)S(1)}, f32[128,128]{1,0:T(8,128)S(1)}, u32[]{:S(2)}, u32[]{:S(2)}) %collective-permute-start.8) | collective-permute-done | bytes 65568 | tf_op jit(solution)/shard_map/ppermute | solution.py:30
  26.2 0.9 %finish.1 = (f32[32,128]{1,0:T(8,128)}, f32[256,128]{1,0:T(8,128)}) custom-call(f32[32,128]{1,0:T(8,128)S(1)} %get-tuple-element.16.own_ref, f32[256,128]{1,0:T(8,128)S(1)} %fusion.left_ref, f32[128,128]{1,0:T(8,128)S(1)} %broadcast_select_fusion.right_ref, f32[256,128]{1,0:T(8,128)S(1)} %fetch.1.prior_ref), custom_call_target="tpu_custom_call" | custom-call | tf_op jit(solution)/shard_map/finish/pallas_call | solution.py:236
  (25 shorter events, 0.2 us)
Async XLA Ops:
  1.5 5.8 %copy-start = (f32[2,128]{1,0:T(2,128)S(1)}, f32[2,128]{1,0:T(2,128)}, u32[]{:S(2)}) copy-start(f32[2,128]{1,0:T(2,128)} %param.7) | copy-start | bytes 3076
  1.5 7.1 %collective-permute-start.2 = (f32[1,40,256]{2,1,0:T(8,128)S(1)}, f32[1,40,256]{2,1,0:T(8,128)S(1)}, u32[]{:S(2)}, u32[]{:S(2)}) collective-permute-start(f32[1,40,256]{2,1,0:T(8,128)S(1)} %bitcast.40), channel_id=1, source_target_pairs={{0,24},{1,25},{2,26},{3,27},{4,28},{5,29},{6,30},{7,31},{8,16},{9,... | collective-permute-start | bytes 122888 | tf_op jit(solution)/shard_map/ppermute | solution.py:30
  6.7 4.9 %collective-permute-start.1 = (f32[1,40,256]{2,1,0:T(8,128)S(1)}, f32[1,40,256]{2,1,0:T(8,128)S(1)}, u32[]{:S(2)}, u32[]{:S(2)}) collective-permute-start(f32[1,40,256]{2,1,0:T(8,128)S(1)} %bitcast.41), channel_id=1, source_target_pairs={{0,16},{1,17},{2,18},{3,19},{4,20},{5,21},{6,22},{7,23},{8,24},{9,... | collective-permute-start | bytes 122888 | tf_op jit(solution)/shard_map/ppermute | solution.py:30
  6.7 4.9 %collective-permute-start = (f32[1,40,256]{2,1,0:T(8,128)S(1)}, f32[1,40,256]{2,1,0:T(8,128)S(1)}, u32[]{:S(2)}, u32[]{:S(2)}) collective-permute-start(f32[1,40,256]{2,1,0:T(8,128)S(1)} %bitcast.42), channel_id=1, source_target_pairs={{0,8},{1,9},{2,10},{3,11},{4,12},{5,13},{6,14},{7,15},{8,0},{9,1},... | collective-permute-start | bytes 122888 | tf_op jit(solution)/shard_map/ppermute | solution.py:30
  11.8 1.3 %collective-permute-start.3 = (f32[144,128]{1,0:T(8,128)S(1)}, f32[144,128]{1,0:T(8,128)S(1)}, u32[]{:S(2)}, u32[]{:S(2)}) collective-permute-start(f32[144,128]{1,0:T(8,128)S(1)} %pad_maximum_fusion.3), channel_id=1, source_target_pairs={{0,1},{1,0},{2,3},{3,2},{4,5},{5,4},{6,7},{7,6},{8,9},{9,8},{10,11... | collective-permute-start | bytes 221192 | tf_op jit(solution)/shard_map/ppermute | solution.py:30
  13.2 5.5 %collective-permute-start.6 = (f32[160,128]{1,0:T(8,128)S(1)}, f32[160,128]{1,0:T(8,128)S(1)}, u32[]{:S(2)}, u32[]{:S(2)}) collective-permute-start(f32[160,128]{1,0:T(8,128)S(1)} %pad_maximum_fusion.2), channel_id=1, source_target_pairs={{0,6},{1,7},{2,4},{3,5},{4,2},{5,3},{6,0},{7,1},{8,14},{9,15},{10,... | collective-permute-start | bytes 245768 | tf_op jit(solution)/shard_map/ppermute | solution.py:30
  15.7 4.7 %collective-permute-start.5 = (f32[160,128]{1,0:T(8,128)S(1)}, f32[160,128]{1,0:T(8,128)S(1)}, u32[]{:S(2)}, u32[]{:S(2)}) collective-permute-start(f32[160,128]{1,0:T(8,128)S(1)} %pad_maximum_fusion.2), channel_id=1, source_target_pairs={{0,4},{1,5},{2,6},{3,7},{4,0},{5,1},{6,2},{7,3},{8,12},{9,13},{10,... | collective-permute-start | bytes 245768 | tf_op jit(solution)/shard_map/ppermute | solution.py:30
  16.2 4.4 %collective-permute-start.4 = (f32[160,128]{1,0:T(8,128)S(1)}, f32[160,128]{1,0:T(8,128)S(1)}, u32[]{:S(2)}, u32[]{:S(2)}) collective-permute-start(f32[160,128]{1,0:T(8,128)S(1)} %pad_maximum_fusion.2), channel_id=1, source_target_pairs={{0,2},{1,3},{2,0},{3,1},{4,6},{5,7},{6,4},{7,5},{8,10},{9,11},{10,... | collective-permute-start | bytes 245768 | tf_op jit(solution)/shard_map/ppermute | solution.py:30
  20.7 3.7 %collective-permute-start.7 = (f32[128,128]{1,0:T(8,128)S(1)}, f32[128,128]{1,0:T(8,128)S(1)}, u32[]{:S(2)}, u32[]{:S(2)}) collective-permute-start(f32[128,128]{1,0:T(8,128)S(1)} %slice_add_fusion), channel_id=1, source_target_pairs={{0,1},{1,0},{2,3},{3,2},{4,5},{5,4},{6,7},{7,6},{8,9},{9,8},{10,11... | collective-permute-start | bytes 196616 | tf_op jit(solution)/shard_map/ppermute | solution.py:30
  20.7 5.4 %collective-permute-start.8 = (f32[128,128]{1,0:T(8,128)S(1)}, f32[128,128]{1,0:T(8,128)S(1)}, u32[]{:S(2)}, u32[]{:S(2)}) collective-permute-start(f32[128,128]{1,0:T(8,128)S(1)} %slice_add_fusion), channel_id=1, source_target_pairs={{0,24},{1,25},{2,16},{3,17},{4,8},{5,9},{6,0},{7,1},{8,2},{9,3},{1... | collective-permute-start | bytes 196616 | tf_op jit(solution)/shard_map/ppermute | solution.py:30

commit v6 on v5

--- a/solution.py
+++ b/solution.py
@@ -41,7 +41,8 @@
 
 def matching(count, home, flip):
     near = sorted(range(count), key=lambda chip: (bin(chip ^ home).count("1"), -chip if flip else chip))
-    far = sorted(range(count), key=lambda plane: -abs(plane - home))
+    far = sorted(set(range(count)) - {home}, key=lambda plane: -abs(plane - home))
+    far.insert(1, home)
     return [plane for _, plane in sorted(zip(near, far))]
 
 
@@ -306,7 +307,7 @@
         return i, j ^ 1
 
     def to_column(i, j):
-        return matching(rows, i, False)[j // 2], 2 * i + j % 2
+        return matching(rows, i, j % 2 == 0)[j // 2], 2 * i + j % 2
 
     half, other_half = fetch_halves(prior_solution, tile)
     blocks = gather(pack(prior_factor, band_factor, band_sites), rows, cols, rows, along_row)

time: 27.2 us -> 26.7 us (0.982)
  the two profiles are of different devices: /device:TPU:0 before, /device:TPU:19 now
where the time goes in v6:
time: 26.7 us; the launch traced here: 26.5 us
  starting transfers between devices  9.87 us (37%)
  waiting for transfers between devices  9.28 us (35%)
  Pallas kernels  5.81 us (22%)
  between operations  0.84 us (3%)
  matrix products  0.49 us (2%)
    ppermute x9, starting transfers between devices, permute(): return lax.ppermute(x, ('row', 'col'), pairs)  9.87 us
    ppermute x9, waiting for transfers between devices, permute(): return lax.ppermute(x, ('row', 'col'), pairs)  9.28 us
    pallas_call x1, Pallas kernels, invert(): pl.pallas_call(body, out_shape=(pltpu.VMEM((tile_rows, size), jnp.float32...  1.95 us
    pallas_call x1, Pallas kernels, fetch_halves(): pl.pallas_call(body, out_shape=(pltpu.VMEM(shape, x.dtype), pltpu.VMEM(sh...  1 us
    pallas_call x1, Pallas kernels, fetch(): pl.pallas_call(body, out_shape=pltpu.VMEM(x.shape, x.dtype), in_specs=[pl...  0.91 us
    pallas_call x1, Pallas kernels, finish(): pl.pallas_call(body, out_shape=(jax.ShapeDtypeStruct(rows_shape, jnp.floa...  0.88 us
    pallas_call x1, Pallas kernels, pack(): pl.pallas_call(body, out_shape=pltpu.VMEM((height + 8, width), jnp.float3...  0.86 us
  transfers between devices with their start and end apart: 9, of which 6 were waited for; matrix products, arithmetic and copies ran while one was open for 2% of the time, Pallas kernels for 15%

profile of v6, /device:TPU:19, one launch (start us, length us, event | category | flops | bytes accessed | tf_op | source)
XLA Modules:
  0.0 26.5 jit_solution(3468371422228496494)
XLA Ops:
  0.6 0.9 %pack.1 = f32[40,256]{1,0:T(8,128)S(1)} custom-call(f32[32,256]{1,0:T(8,128)} %factor_ref.1, f32[16,32]{1,0:T(8,128)} %bitcast.50, f32[2,32]{1,0:T(2,128)} %sites_ref.1), custom_call_target="tpu_custom_call" | custom-call | tf_op jit(solution)/shard_map/pack/pallas_call | solution.py:278
  1.5 0.0 copy-start
  1.5 0.2 collective-permute-start.2
  1.7 3.2 %collective-permute-start.1 = (f32[1,40,256]{2,1,0:T(8,128)S(1)}, f32[1,40,256]{2,1,0:T(8,128)S(1)}, u32[]{:S(2)}, u32[]{:S(2)}) collective-permute-start(f32[1,40,256]{2,1,0:T(8,128)S(1)} %bitcast.41), channel_id=1, source_target_pairs={{0,16},{1,17},{2,18},{3,19},{4,20},{5,21},{6,22},{7,23},{8,24},{9,... | collective-permute-start | bytes 122888 | tf_op jit(solution)/shard_map/ppermute | solution.py:30
  5.0 1.0 %fetch_halves.1 = (f32[256,128]{1,0:T(8,128)S(1)}, f32[256,128]{1,0:T(8,128)S(1)}) custom-call(f32[256,256]{1,0:T(8,128)} %x_ref.2), custom_call_target="tpu_custom_call" | custom-call | tf_op jit(solution)/shard_map/fetch_halves/pallas_call | solution.py:172
  6.0 0.0 collective-permute-done.2
  6.0 0.9 %collective-permute-done.1 = f32[1,40,256]{2,1,0:T(8,128)S(1)} collective-permute-done((f32[1,40,256]{2,1,0:T(8,128)S(1)}, f32[1,40,256]{2,1,0:T(8,128)S(1)}, u32[]{:S(2)}, u32[]{:S(2)}) %collective-permute-start.1) | collective-permute-done | bytes 40992 | tf_op jit(solution)/shard_map/ppermute | solution.py:30
  6.9 1.2 %collective-permute-done = f32[1,40,256]{2,1,0:T(8,128)S(1)} collective-permute-done((f32[1,40,256]{2,1,0:T(8,128)S(1)}, f32[1,40,256]{2,1,0:T(8,128)S(1)}, u32[]{:S(2)}, u32[]{:S(2)}) %collective-permute-start) | collective-permute-done | bytes 40992 | tf_op jit(solution)/shard_map/ppermute | solution.py:30
  8.1 0.2 first_product.1
  8.4 2.2 %collective-permute-start.3 = (f32[144,128]{1,0:T(8,128)S(1)}, f32[144,128]{1,0:T(8,128)S(1)}, u32[]{:S(2)}, u32[]{:S(2)}) collective-permute-start(f32[144,128]{1,0:T(8,128)S(1)} %pad_maximum_fusion.3), channel_id=1, source_target_pairs={{0,1},{1,0},{2,3},{3,2},{4,5},{5,4},{6,7},{7,6},{8,9},{9,8},{10,11... | collective-permute-start | bytes 221192 | tf_op jit(solution)/shard_map/ppermute | solution.py:30
  10.5 0.2 convolution_subtract_fusion
  10.7 0.7 %collective-permute-done.3 = f32[144,128]{1,0:T(8,128)S(1)} collective-permute-done((f32[144,128]{1,0:T(8,128)S(1)}, f32[144,128]{1,0:T(8,128)S(1)}, u32[]{:S(2)}, u32[]{:S(2)}) %collective-permute-start.3) | collective-permute-done | bytes 73760 | tf_op jit(solution)/shard_map/ppermute | solution.py:30
  11.5 1.3 %collective-permute-start.6 = (f32[160,128]{1,0:T(8,128)S(1)}, f32[160,128]{1,0:T(8,128)S(1)}, u32[]{:S(2)}, u32[]{:S(2)}) collective-permute-start(f32[160,128]{1,0:T(8,128)S(1)} %pad_maximum_fusion.2), channel_id=1, source_target_pairs={{0,6},{1,7},{2,4},{3,5},{4,2},{5,3},{6,0},{7,1},{8,14},{9,15},{10,... | collective-permute-start | bytes 245768 | tf_op jit(solution)/shard_map/ppermute | solution.py:30
  12.7 0.2 collective-permute-start.5
  13.0 1.2 %collective-permute-start.4 = (f32[160,128]{1,0:T(8,128)S(1)}, f32[160,128]{1,0:T(8,128)S(1)}, u32[]{:S(2)}, u32[]{:S(2)}) collective-permute-start(f32[160,128]{1,0:T(8,128)S(1)} %pad_maximum_fusion.2), channel_id=1, source_target_pairs={{0,2},{1,3},{2,0},{3,1},{4,6},{5,7},{6,4},{7,5},{8,10},{9,11},{10,... | collective-permute-start | bytes 245768 | tf_op jit(solution)/shard_map/ppermute | solution.py:30
  14.2 0.9 %fetch.1.prior_ref = f32[256,128]{1,0:T(8,128)S(1)} custom-call(f32[256,128]{1,0:T(8,128)} %x_ref.3), custom_call_target="tpu_custom_call" | custom-call | tf_op jit(solution)/shard_map/fetch/pallas_call | solution.py:146
  15.1 1.0 %collective-permute-done.6 = f32[160,128]{1,0:T(8,128)S(1)} collective-permute-done((f32[160,128]{1,0:T(8,128)S(1)}, f32[160,128]{1,0:T(8,128)S(1)}, u32[]{:S(2)}, u32[]{:S(2)}) %collective-permute-start.6) | collective-permute-done | bytes 81952 | tf_op jit(solution)/shard_map/ppermute | solution.py:30
  16.1 2.5 %collective-permute-done.5 = f32[160,128]{1,0:T(8,128)S(1)} collective-permute-done((f32[160,128]{1,0:T(8,128)S(1)}, f32[160,128]{1,0:T(8,128)S(1)}, u32[]{:S(2)}, u32[]{:S(2)}) %collective-permute-start.5) | collective-permute-done | bytes 81952 | tf_op jit(solution)/shard_map/ppermute | solution.py:30
  18.6 0.6 %collective-permute-start.7 = (f32[128,128]{1,0:T(8,128)S(1)}, f32[128,128]{1,0:T(8,128)S(1)}, u32[]{:S(2)}, u32[]{:S(2)}) collective-permute-start(f32[128,128]{1,0:T(8,128)S(1)} %slice_add_fusion), channel_id=1, source_target_pairs={{0,1},{1,0},{2,3},{3,2},{4,5},{5,4},{6,7},{7,6},{8,9},{9,8},{10,11... | collective-permute-start | bytes 196616 | tf_op jit(solution)/shard_map/ppermute | solution.py:30
  19.2 0.9 %collective-permute-start.8 = (f32[128,128]{1,0:T(8,128)S(1)}, f32[128,128]{1,0:T(8,128)S(1)}, u32[]{:S(2)}, u32[]{:S(2)}) collective-permute-start(f32[128,128]{1,0:T(8,128)S(1)} %slice_add_fusion), channel_id=1, source_target_pairs={{0,24},{1,25},{2,16},{3,1},{4,0},{5,17},{6,8},{7,9},{8,2},{9,11},{... | collective-permute-start | bytes 196616 | tf_op jit(solution)/shard_map/ppermute | solution.py:30
  20.2 1.9 %invert.1 = (f32[32,128]{1,0:T(8,128)S(1)}, f32[128,128]{1,0:T(8,128)S(1)}) custom-call(f32[128,128]{1,0:T(8,128)S(1)} %bitcast.39), custom_call_target="tpu_custom_call" | custom-call | tf_op jit(solution)/shard_map/invert/pallas_call | solution.py:126
  22.2 0.3 %fusion.left_ref = f32[256,128]{1,0:T(8,128)S(1)} fusion(f32[128,128]{1,0:T(8,128)S(1)} %get-tuple-element.17, f32[128,128]{1,0:T(8,128)S(1)} %slice_bitcast_fusion, f32[128,128]{1,0:T(8,128)S(1)} %slice_bitcast_fusion.1), kind=kOutput, calls=%fused_computation.4 | convolution fusion | flops 25198592 | bytes 327680 | tf_op jit(solution)/shard_map/dot_general | solution.py:21
  22.5 3.0 %collective-permute-done.8 = f32[128,128]{1,0:T(8,128)S(1)} collective-permute-done((f32[128,128]{1,0:T(8,128)S(1)}, f32[128,128]{1,0:T(8,128)S(1)}, u32[]{:S(2)}, u32[]{:S(2)}) %collective-permute-start.8) | collective-permute-done | bytes 65568 | tf_op jit(solution)/shard_map/ppermute | solution.py:30
  25.6 0.9 %finish.1 = (f32[32,128]{1,0:T(8,128)}, f32[256,128]{1,0:T(8,128)}) custom-call(f32[32,128]{1,0:T(8,128)S(1)} %get-tuple-element.16.own_ref, f32[256,128]{1,0:T(8,128)S(1)} %fusion.left_ref, f32[128,128]{1,0:T(8,128)S(1)} %broadcast_select_fusion.right_ref, f32[256,128]{1,0:T(8,128)S(1)} %fetch.1.prior_ref), custom_call_target="tpu_custom_call" | custom-call | tf_op jit(solution)/shard_map/finish/pallas_call | solution.py:237
  (25 shorter events, 0.2 us)
Async XLA Ops:
  1.5 3.5 %copy-start = (f32[2,128]{1,0:T(2,128)S(1)}, f32[2,128]{1,0:T(2,128)}, u32[]{:S(2)}) copy-start(f32[2,128]{1,0:T(2,128)} %param.7) | copy-start | bytes 3076
  1.5 4.5 %collective-permute-start.2 = (f32[1,40,256]{2,1,0:T(8,128)S(1)}, f32[1,40,256]{2,1,0:T(8,128)S(1)}, u32[]{:S(2)}, u32[]{:S(2)}) collective-permute-start(f32[1,40,256]{2,1,0:T(8,128)S(1)} %bitcast.40), channel_id=1, source_target_pairs={{0,24},{1,25},{2,26},{3,27},{4,28},{5,29},{6,30},{7,31},{8,16},{9,... | collective-permute-start | bytes 122888 | tf_op jit(solution)/shard_map/ppermute | solution.py:30
  1.7 5.1 %collective-permute-start.1 = (f32[1,40,256]{2,1,0:T(8,128)S(1)}, f32[1,40,256]{2,1,0:T(8,128)S(1)}, u32[]{:S(2)}, u32[]{:S(2)}) collective-permute-start(f32[1,40,256]{2,1,0:T(8,128)S(1)} %bitcast.41), channel_id=1, source_target_pairs={{0,16},{1,17},{2,18},{3,19},{4,20},{5,21},{6,22},{7,23},{8,24},{9,... | collective-permute-start | bytes 122888 | tf_op jit(solution)/shard_map/ppermute | solution.py:30
  5.0 3.1 %collective-permute-start = (f32[1,40,256]{2,1,0:T(8,128)S(1)}, f32[1,40,256]{2,1,0:T(8,128)S(1)}, u32[]{:S(2)}, u32[]{:S(2)}) collective-permute-start(f32[1,40,256]{2,1,0:T(8,128)S(1)} %bitcast.42), channel_id=1, source_target_pairs={{0,8},{1,9},{2,10},{3,11},{4,12},{5,13},{6,14},{7,15},{8,0},{9,1},... | collective-permute-start | bytes 122888 | tf_op jit(solution)/shard_map/ppermute | solution.py:30
  8.4 3.1 %collective-permute-start.3 = (f32[144,128]{1,0:T(8,128)S(1)}, f32[144,128]{1,0:T(8,128)S(1)}, u32[]{:S(2)}, u32[]{:S(2)}) collective-permute-start(f32[144,128]{1,0:T(8,128)S(1)} %pad_maximum_fusion.3), channel_id=1, source_target_pairs={{0,1},{1,0},{2,3},{3,2},{4,5},{5,4},{6,7},{7,6},{8,9},{9,8},{10,11... | collective-permute-start | bytes 221192 | tf_op jit(solution)/shard_map/ppermute | solution.py:30
  11.5 4.6 %collective-permute-start.6 = (f32[160,128]{1,0:T(8,128)S(1)}, f32[160,128]{1,0:T(8,128)S(1)}, u32[]{:S(2)}, u32[]{:S(2)}) collective-permute-start(f32[160,128]{1,0:T(8,128)S(1)} %pad_maximum_fusion.2), channel_id=1, source_target_pairs={{0,6},{1,7},{2,4},{3,5},{4,2},{5,3},{6,0},{7,1},{8,14},{9,15},{10,... | collective-permute-start | bytes 245768 | tf_op jit(solution)/shard_map/ppermute | solution.py:30
  12.7 5.8 %collective-permute-start.5 = (f32[160,128]{1,0:T(8,128)S(1)}, f32[160,128]{1,0:T(8,128)S(1)}, u32[]{:S(2)}, u32[]{:S(2)}) collective-permute-start(f32[160,128]{1,0:T(8,128)S(1)} %pad_maximum_fusion.2), channel_id=1, source_target_pairs={{0,4},{1,5},{2,6},{3,7},{4,0},{5,1},{6,2},{7,3},{8,12},{9,13},{10,... | collective-permute-start | bytes 245768 | tf_op jit(solution)/shard_map/ppermute | solution.py:30
  13.0 5.6 %collective-permute-start.4 = (f32[160,128]{1,0:T(8,128)S(1)}, f32[160,128]{1,0:T(8,128)S(1)}, u32[]{:S(2)}, u32[]{:S(2)}) collective-permute-start(f32[160,128]{1,0:T(8,128)S(1)} %pad_maximum_fusion.2), channel_id=1, source_target_pairs={{0,2},{1,3},{2,0},{3,1},{4,6},{5,7},{6,4},{7,5},{8,10},{9,11},{10,... | collective-permute-start | bytes 245768 | tf_op jit(solution)/shard_map/ppermute | solution.py:30
  18.6 3.6 %collective-permute-start.7 = (f32[128,128]{1,0:T(8,128)S(1)}, f32[128,128]{1,0:T(8,128)S(1)}, u32[]{:S(2)}, u32[]{:S(2)}) collective-permute-start(f32[128,128]{1,0:T(8,128)S(1)} %slice_add_fusion), channel_id=1, source_target_pairs={{0,1},{1,0},{2,3},{3,2},{4,5},{5,4},{6,7},{7,6},{8,9},{9,8},{10,11... | collective-permute-start | bytes 196616 | tf_op jit(solution)/shard_map/ppermute | solution.py:30
  19.2 6.4 %collective-permute-start.8 = (f32[128,128]{1,0:T(8,128)S(1)}, f32[128,128]{1,0:T(8,128)S(1)}, u32[]{:S(2)}, u32[]{:S(2)}) collective-permute-start(f32[128,128]{1,0:T(8,128)S(1)} %slice_add_fusion), channel_id=1, source_target_pairs={{0,24},{1,25},{2,16},{3,1},{4,0},{5,17},{6,8},{7,9},{8,2},{9,11},{... | collective-permute-start | bytes 196616 | tf_op jit(solution)/shard_map/ppermute | solution.py:30

commit v7 on v6

--- a/solution.py
+++ b/solution.py
@@ -213,6 +213,26 @@
     )(*[pltpu.with_memory_space_constraint(x, pltpu.VMEM) for x in (blocks, theirs)])
 
 
+def left_product(rest, other, normal):
+    band, tile = rest.shape
+
+    def body(rest_ref, other_ref, normal_ref, out_ref):
+        k = lax.axis_index("col") % 2
+        right = split(normal_ref[...])
+        for ref, half in ((rest_ref, k), (other_ref, 1 - k)):
+            start = pl.multiple_of(half * tile, tile)
+            out_ref[pl.ds(start, tile)] = dot3(split(ref[...].T), right)
+
+    vmem = pl.BlockSpec(memory_space=pltpu.VMEM)
+    return pl.pallas_call(
+        body,
+        out_shape=pltpu.VMEM((2 * tile, band), jnp.float32),
+        in_specs=[vmem] * 3,
+        out_specs=vmem,
+        name="left_product",
+    )(*[pltpu.with_memory_space_constraint(x, pltpu.VMEM) for x in (rest, other, normal)])
+
+
 def finish(own, left, right, prior_covariance):
     tall, tile = prior_covariance.shape
     pieces = 2
@@ -330,11 +350,8 @@
         inverse = upper_inverse(triangle, dot)
         normal = dot(inverse, inverse, ((1,), (1,)))
         own = lax.dynamic_slice_in_dim(inverse, r * tile_rows, tile_rows, 1).T
-    first = ((0,), (0,))
-    both = natural(jnp.stack([rest, rest_other]), k)
-    left = jnp.concatenate([both[0], both[1]], axis=1)
     prior = fetch(prior_covariance)
-    left = dot(left, normal, first, HIGH)
+    left = left_product(rest, rest_other, normal)
     return finish(own, left, jnp.where(q == r, rest, moved), prior)
 
 

time: 26.7 us -> 27 us (1.011)
  waiting for transfers between devices: 9.28 us -> 9.66 us
  matrix products: 0.49 us -> 0.2 us
  Pallas kernels: 5.81 us -> 6.08 us
    ppermute x9, waiting for transfers between devices: 9.28 us -> 9.66 us  [permute(): return lax.ppermute(x, ('row', 'col'), pairs)]
    dot_general x2 -> x1, matrix products: 0.49 us -> 0.2 us  [dot(): lax.dot_general(a, b, (contract, ((), ())), precision=precision, preferre...]
    pallas_call x0 -> x1, Pallas kernels: none -> 0.27 us  [left_product(): pl.pallas_call(body, out_shape=pltpu.VMEM((2 * tile, band), jnp.float32),...]
  transfers between devices with their start and end apart: 9 -> 9, of which waited for: 6 -> 6; matrix products, arithmetic and copies ran while one was open for 2% -> 1% of each run, Pallas kernels for 15% -> 14%
where the time goes in v7:
time: 27 us; the launch traced here: 26.8 us
  starting transfers between devices  9.87 us (37%)
  waiting for transfers between devices  9.66 us (36%)
  Pallas kernels  6.08 us (23%)
  between operations  0.81 us (3%)
    ppermute x9, starting transfers between devices, permute(): return lax.ppermute(x, ('row', 'col'), pairs)  9.87 us
    ppermute x9, waiting for transfers between devices, permute(): return lax.ppermute(x, ('row', 'col'), pairs)  9.66 us
    pallas_call x1, Pallas kernels, invert(): pl.pallas_call(body, out_shape=(pltpu.VMEM((tile_rows, size), jnp.float32...  1.95 us
    pallas_call x1, Pallas kernels, fetch_halves(): pl.pallas_call(body, out_shape=(pltpu.VMEM(shape, x.dtype), pltpu.VMEM(sh...  1 us
    pallas_call x1, Pallas kernels, fetch(): pl.pallas_call(body, out_shape=pltpu.VMEM(x.shape, x.dtype), in_specs=[pl...  0.91 us
    pallas_call x1, Pallas kernels, finish(): pl.pallas_call(body, out_shape=(jax.ShapeDtypeStruct(rows_shape, jnp.floa...  0.88 us
    pallas_call x1, Pallas kernels, pack(): pl.pallas_call(body, out_shape=pltpu.VMEM((height + 8, width), jnp.float3...  0.86 us
  transfers between devices with their start and end apart: 9, of which 6 were waited for; matrix products, arithmetic and copies ran while one was open for 1% of the time, Pallas kernels for 14%

profile of v7, /device:TPU:19, one launch (start us, length us, event | category | flops | bytes accessed | tf_op | source)
XLA Modules:
  0.0 26.8 jit_solution(8895967190206805454)
XLA Ops:
  0.6 0.9 %pack.1 = f32[40,256]{1,0:T(8,128)S(1)} custom-call(f32[32,256]{1,0:T(8,128)} %factor_ref.1, f32[16,32]{1,0:T(8,128)} %bitcast.36, f32[2,32]{1,0:T(2,128)} %sites_ref.1), custom_call_target="tpu_custom_call" | custom-call | tf_op jit(solution)/shard_map/pack/pallas_call | solution.py:298
  1.5 0.0 copy-start
  1.5 0.2 collective-permute-start.2
  1.7 3.2 %collective-permute-start.1 = (f32[1,40,256]{2,1,0:T(8,128)S(1)}, f32[1,40,256]{2,1,0:T(8,128)S(1)}, u32[]{:S(2)}, u32[]{:S(2)}) collective-permute-start(f32[1,40,256]{2,1,0:T(8,128)S(1)} %bitcast.29), channel_id=1, source_target_pairs={{0,16},{1,17},{2,18},{3,19},{4,20},{5,21},{6,22},{7,23},{8,24},{9,... | collective-permute-start | bytes 122888 | tf_op jit(solution)/shard_map/ppermute | solution.py:30
  5.0 1.0 %fetch_halves.1 = (f32[256,128]{1,0:T(8,128)S(1)}, f32[256,128]{1,0:T(8,128)S(1)}) custom-call(f32[256,256]{1,0:T(8,128)} %x_ref.2), custom_call_target="tpu_custom_call" | custom-call | tf_op jit(solution)/shard_map/fetch_halves/pallas_call | solution.py:172
  6.0 0.0 collective-permute-done.2
  6.0 0.9 %collective-permute-done.1 = f32[1,40,256]{2,1,0:T(8,128)S(1)} collective-permute-done((f32[1,40,256]{2,1,0:T(8,128)S(1)}, f32[1,40,256]{2,1,0:T(8,128)S(1)}, u32[]{:S(2)}, u32[]{:S(2)}) %collective-permute-start.1) | collective-permute-done | bytes 40992 | tf_op jit(solution)/shard_map/ppermute | solution.py:30
  6.9 1.2 %collective-permute-done = f32[1,40,256]{2,1,0:T(8,128)S(1)} collective-permute-done((f32[1,40,256]{2,1,0:T(8,128)S(1)}, f32[1,40,256]{2,1,0:T(8,128)S(1)}, u32[]{:S(2)}, u32[]{:S(2)}) %collective-permute-start) | collective-permute-done | bytes 40992 | tf_op jit(solution)/shard_map/ppermute | solution.py:30
  8.1 0.2 first_product.1
  8.4 2.2 %collective-permute-start.3 = (f32[144,128]{1,0:T(8,128)S(1)}, f32[144,128]{1,0:T(8,128)S(1)}, u32[]{:S(2)}, u32[]{:S(2)}) collective-permute-start(f32[144,128]{1,0:T(8,128)S(1)} %pad_maximum_fusion.2), channel_id=1, source_target_pairs={{0,1},{1,0},{2,3},{3,2},{4,5},{5,4},{6,7},{7,6},{8,9},{9,8},{10,11... | collective-permute-start | bytes 221192 | tf_op jit(solution)/shard_map/ppermute | solution.py:30
  10.5 0.2 convolution_subtract_fusion
  10.7 0.7 %collective-permute-done.3 = f32[144,128]{1,0:T(8,128)S(1)} collective-permute-done((f32[144,128]{1,0:T(8,128)S(1)}, f32[144,128]{1,0:T(8,128)S(1)}, u32[]{:S(2)}, u32[]{:S(2)}) %collective-permute-start.3) | collective-permute-done | bytes 73760 | tf_op jit(solution)/shard_map/ppermute | solution.py:30
  11.5 1.3 %collective-permute-start.6 = (f32[160,128]{1,0:T(8,128)S(1)}, f32[160,128]{1,0:T(8,128)S(1)}, u32[]{:S(2)}, u32[]{:S(2)}) collective-permute-start(f32[160,128]{1,0:T(8,128)S(1)} %pad_maximum_fusion.1), channel_id=1, source_target_pairs={{0,6},{1,7},{2,4},{3,5},{4,2},{5,3},{6,0},{7,1},{8,14},{9,15},{10,... | collective-permute-start | bytes 245768 | tf_op jit(solution)/shard_map/ppermute | solution.py:30
  12.7 0.2 collective-permute-start.5
  13.0 1.2 %collective-permute-start.4 = (f32[160,128]{1,0:T(8,128)S(1)}, f32[160,128]{1,0:T(8,128)S(1)}, u32[]{:S(2)}, u32[]{:S(2)}) collective-permute-start(f32[160,128]{1,0:T(8,128)S(1)} %pad_maximum_fusion.1), channel_id=1, source_target_pairs={{0,2},{1,3},{2,0},{3,1},{4,6},{5,7},{6,4},{7,5},{8,10},{9,11},{10,... | collective-permute-start | bytes 245768 | tf_op jit(solution)/shard_map/ppermute | solution.py:30
  14.2 0.9 %fetch.1.prior_ref = f32[256,128]{1,0:T(8,128)S(1)} custom-call(f32[256,128]{1,0:T(8,128)} %x_ref.3), custom_call_target="tpu_custom_call" | custom-call | tf_op jit(solution)/shard_map/fetch/pallas_call | solution.py:146
  15.1 1.0 %collective-permute-done.6 = f32[160,128]{1,0:T(8,128)S(1)} collective-permute-done((f32[160,128]{1,0:T(8,128)S(1)}, f32[160,128]{1,0:T(8,128)S(1)}, u32[]{:S(2)}, u32[]{:S(2)}) %collective-permute-start.6) | collective-permute-done | bytes 81952 | tf_op jit(solution)/shard_map/ppermute | solution.py:30
  16.1 2.5 %collective-permute-done.5 = f32[160,128]{1,0:T(8,128)S(1)} collective-permute-done((f32[160,128]{1,0:T(8,128)S(1)}, f32[160,128]{1,0:T(8,128)S(1)}, u32[]{:S(2)}, u32[]{:S(2)}) %collective-permute-start.5) | collective-permute-done | bytes 81952 | tf_op jit(solution)/shard_map/ppermute | solution.py:30
  18.6 0.6 %collective-permute-start.7 = (f32[128,128]{1,0:T(8,128)S(1)}, f32[128,128]{1,0:T(8,128)S(1)}, u32[]{:S(2)}, u32[]{:S(2)}) collective-permute-start(f32[128,128]{1,0:T(8,128)S(1)} %slice_add_fusion.rest_ref), channel_id=1, source_target_pairs={{0,1},{1,0},{2,3},{3,2},{4,5},{5,4},{6,7},{7,6},{8,9},{9,8},{10,11... | collective-permute-start | bytes 196616 | tf_op jit(solution)/shard_map/ppermute | solution.py:30
  19.2 0.9 %collective-permute-start.8 = (f32[128,128]{1,0:T(8,128)S(1)}, f32[128,128]{1,0:T(8,128)S(1)}, u32[]{:S(2)}, u32[]{:S(2)}) collective-permute-start(f32[128,128]{1,0:T(8,128)S(1)} %slice_add_fusion.rest_ref), channel_id=1, source_target_pairs={{0,24},{1,25},{2,16},{3,1},{4,0},{5,17},{6,8},{7,9},{8,2},{9,11},{... | collective-permute-start | bytes 196616 | tf_op jit(solution)/shard_map/ppermute | solution.py:30
  20.2 1.9 %invert.1 = (f32[32,128]{1,0:T(8,128)S(1)}, f32[128,128]{1,0:T(8,128)S(1)}) custom-call(f32[128,128]{1,0:T(8,128)S(1)} %bitcast.27), custom_call_target="tpu_custom_call" | custom-call | tf_op jit(solution)/shard_map/invert/pallas_call | solution.py:126
  22.1 3.4 %collective-permute-done.8 = f32[128,128]{1,0:T(8,128)S(1)} collective-permute-done((f32[128,128]{1,0:T(8,128)S(1)}, f32[128,128]{1,0:T(8,128)S(1)}, u32[]{:S(2)}, u32[]{:S(2)}) %collective-permute-start.8) | collective-permute-done | bytes 65568 | tf_op jit(solution)/shard_map/ppermute | solution.py:30
  25.6 0.3 %left_product.1.left_ref = f32[256,128]{1,0:T(8,128)S(1)} custom-call(f32[128,128]{1,0:T(8,128)S(1)} %slice_add_fusion.rest_ref, f32[128,128]{1,0:T(8,128)S(1)} %collective-permute-done.7.other_ref, f32[128,128]{1,0:T(8,128)S(1)} %get-tuple-element.17.normal_ref), custom_call_target="tpu_custom_call" | custom-call | tf_op jit(solution)/shard_map/left_product/pallas_call | solution.py:227
  25.9 0.9 %finish.1 = (f32[32,128]{1,0:T(8,128)}, f32[256,128]{1,0:T(8,128)}) custom-call(f32[32,128]{1,0:T(8,128)S(1)} %get-tuple-element.16.own_ref, f32[256,128]{1,0:T(8,128)S(1)} %left_product.1.left_ref, f32[128,128]{1,0:T(8,128)S(1)} %broadcast_select_fusion.right_ref, f32[256,128]{1,0:T(8,128)S(1)} %fetch.1.prior_ref), custom_call_target="tpu_custom_call" | custom-call | tf_op jit(solution)/shard_map/finish/pallas_call | solution.py:257
  (21 shorter events, 0.1 us)
Async XLA Ops:
  1.5 3.5 %copy-start = (f32[2,128]{1,0:T(2,128)S(1)}, f32[2,128]{1,0:T(2,128)}, u32[]{:S(2)}) copy-start(f32[2,128]{1,0:T(2,128)} %param.7) | copy-start | bytes 3076
  1.5 4.5 %collective-permute-start.2 = (f32[1,40,256]{2,1,0:T(8,128)S(1)}, f32[1,40,256]{2,1,0:T(8,128)S(1)}, u32[]{:S(2)}, u32[]{:S(2)}) collective-permute-start(f32[1,40,256]{2,1,0:T(8,128)S(1)} %bitcast.28), channel_id=1, source_target_pairs={{0,24},{1,25},{2,26},{3,27},{4,28},{5,29},{6,30},{7,31},{8,16},{9,... | collective-permute-start | bytes 122888 | tf_op jit(solution)/shard_map/ppermute | solution.py:30
  1.7 5.1 %collective-permute-start.1 = (f32[1,40,256]{2,1,0:T(8,128)S(1)}, f32[1,40,256]{2,1,0:T(8,128)S(1)}, u32[]{:S(2)}, u32[]{:S(2)}) collective-permute-start(f32[1,40,256]{2,1,0:T(8,128)S(1)} %bitcast.29), channel_id=1, source_target_pairs={{0,16},{1,17},{2,18},{3,19},{4,20},{5,21},{6,22},{7,23},{8,24},{9,... | collective-permute-start | bytes 122888 | tf_op jit(solution)/shard_map/ppermute | solution.py:30
  5.0 3.1 %collective-permute-start = (f32[1,40,256]{2,1,0:T(8,128)S(1)}, f32[1,40,256]{2,1,0:T(8,128)S(1)}, u32[]{:S(2)}, u32[]{:S(2)}) collective-permute-start(f32[1,40,256]{2,1,0:T(8,128)S(1)} %bitcast.30), channel_id=1, source_target_pairs={{0,8},{1,9},{2,10},{3,11},{4,12},{5,13},{6,14},{7,15},{8,0},{9,1},... | collective-permute-start | bytes 122888 | tf_op jit(solution)/shard_map/ppermute | solution.py:30
  8.4 3.1 %collective-permute-start.3 = (f32[144,128]{1,0:T(8,128)S(1)}, f32[144,128]{1,0:T(8,128)S(1)}, u32[]{:S(2)}, u32[]{:S(2)}) collective-permute-start(f32[144,128]{1,0:T(8,128)S(1)} %pad_maximum_fusion.2), channel_id=1, source_target_pairs={{0,1},{1,0},{2,3},{3,2},{4,5},{5,4},{6,7},{7,6},{8,9},{9,8},{10,11... | collective-permute-start | bytes 221192 | tf_op jit(solution)/shard_map/ppermute | solution.py:30
  11.5 4.6 %collective-permute-start.6 = (f32[160,128]{1,0:T(8,128)S(1)}, f32[160,128]{1,0:T(8,128)S(1)}, u32[]{:S(2)}, u32[]{:S(2)}) collective-permute-start(f32[160,128]{1,0:T(8,128)S(1)} %pad_maximum_fusion.1), channel_id=1, source_target_pairs={{0,6},{1,7},{2,4},{3,5},{4,2},{5,3},{6,0},{7,1},{8,14},{9,15},{10,... | collective-permute-start | bytes 245768 | tf_op jit(solution)/shard_map/ppermute | solution.py:30
  12.7 5.8 %collective-permute-start.5 = (f32[160,128]{1,0:T(8,128)S(1)}, f32[160,128]{1,0:T(8,128)S(1)}, u32[]{:S(2)}, u32[]{:S(2)}) collective-permute-start(f32[160,128]{1,0:T(8,128)S(1)} %pad_maximum_fusion.1), channel_id=1, source_target_pairs={{0,4},{1,5},{2,6},{3,7},{4,0},{5,1},{6,2},{7,3},{8,12},{9,13},{10,... | collective-permute-start | bytes 245768 | tf_op jit(solution)/shard_map/ppermute | solution.py:30
  13.0 5.6 %collective-permute-start.4 = (f32[160,128]{1,0:T(8,128)S(1)}, f32[160,128]{1,0:T(8,128)S(1)}, u32[]{:S(2)}, u32[]{:S(2)}) collective-permute-start(f32[160,128]{1,0:T(8,128)S(1)} %pad_maximum_fusion.1), channel_id=1, source_target_pairs={{0,2},{1,3},{2,0},{3,1},{4,6},{5,7},{6,4},{7,5},{8,10},{9,11},{10,... | collective-permute-start | bytes 245768 | tf_op jit(solution)/shard_map/ppermute | solution.py:30
  18.6 7.0 %collective-permute-start.7 = (f32[128,128]{1,0:T(8,128)S(1)}, f32[128,128]{1,0:T(8,128)S(1)}, u32[]{:S(2)}, u32[]{:S(2)}) collective-permute-start(f32[128,128]{1,0:T(8,128)S(1)} %slice_add_fusion.rest_ref), channel_id=1, source_target_pairs={{0,1},{1,0},{2,3},{3,2},{4,5},{5,4},{6,7},{7,6},{8,9},{9,8},{10,11... | collective-permute-start | bytes 196616 | tf_op jit(solution)/shard_map/ppermute | solution.py:30
  19.2 6.4 %collective-permute-start.8 = (f32[128,128]{1,0:T(8,128)S(1)}, f32[128,128]{1,0:T(8,128)S(1)}, u32[]{:S(2)}, u32[]{:S(2)}) collective-permute-start(f32[128,128]{1,0:T(8,128)S(1)} %slice_add_fusion.rest_ref), channel_id=1, source_target_pairs={{0,24},{1,25},{2,16},{3,1},{4,0},{5,17},{6,8},{7,9},{8,2},{9,11},{... | collective-permute-start | bytes 196616 | tf_op jit(solution)/shard_map/ppermute | solution.py:30
